TPU v7x, 768 devices: a whole 4x8x12 slice. The times are simulated.
768 devices in a mesh: slab: 12 (over z), sub: 64 (over y, x, core).
Axes of the slice: x: 4, y: 8, z: 12, core: 2. Of those that a mesh axis runs over, the one named last changes fastest.
Arguments:
- near_null: float32 [18, 393216], P(None, ('slab', 'sub')), may hold values from -48 to 48
- aggregates: int32 [393216], P(('slab', 'sub')), may hold values from 0 to 63
- diag_block: float32 [9, 393216], P(None, ('slab', 'sub')), may hold values from -1 to 12, as said below
- off_blocks: float32 [26, 9, 393216], P(None, None, ('slab', 'sub')), may hold values from -18 to 18
- columns: int32 [26, 393216], P(None, ('slab', 'sub')), may hold values from 0 to 767, as said below
- sends: int32 [4, 49152], P(None, ('slab', 'sub')), may hold values from 0 to 511
- start_vector: float32 [3, 393216], P(None, ('slab', 'sub')), may hold values from -18 to 18
Outputs:
- prolong_off: bfloat16 [26, 18, 393216], P(None, None, ('slab', 'sub'))
- prolong_self: bfloat16 [18, 393216], P(None, ('slab', 'sub'))
- rho: float32 [], replicated
Inputs may be any that keep to these rules, and one draw needn't show every extreme that they name: `diag_block`: each block, read as 3x3 row-major, is symmetric with diagonal entries between 6 and 12 and off-diagonal entries between -1 and 1. `columns`: entries below 512 name a node of the same device; an entry c of 512 or more names ghost slot c - 512. Row e lists, for each device, the local rows it sends to its neighbour at sub + 1, sub - 1, slab + 1, slab - 1 for e = 0, 1, 2, 3. `aggregates`: aggregates lie within one device.
All inputs are finite; a program needn't handle non-finite values.
Results may differ from a plain program's by a relative error of at most 0.001.
Values sent between devices are 32-bit elements; how exact they have to be, the bound alone decides.
No kernel may reach another device: no remote copies, remote signals or barrier semaphores. Data moves between devices by JAX's collectives and lax.ppermute only.
A program may use at most 32 MiB of HBM per device.

v0:
```python
import functools

import jax
import jax.numpy as jnp
from jax import lax
from jax.experimental import pallas as pl
from jax.experimental.pallas import tpu as pltpu
from jax.sharding import Mesh
from jax.sharding import PartitionSpec as P

ITERS = 8
OMEGA = 4.0 / 3.0
SUB = ("sub_0", "sub_1", "sub_2")
SLAB_SUB = ("slab", "sub_0", "sub_1", "sub_2")
LANES = 128
F32 = jnp.float32
VM = pl.BlockSpec(memory_space=pltpu.VMEM)


def lanes(group):
    return slice(group * LANES, (group + 1) * LANES)


def pick(sources, low, high):
    result = jnp.take_along_axis(sources[0], low, axis=1, mode="promise_in_bounds")
    for group in range(1, len(sources)):
        found = jnp.take_along_axis(sources[group], low, axis=1, mode="promise_in_bounds")
        result = jnp.where(high == group, found, result)
    return result


def spread(row):
    return jnp.broadcast_to(row, (8, LANES))


def pack_rows(table_ref, tiles, send_ref, pay_refs):
    for pay_ref, first in zip(pay_refs, (0, 1)):
        index = spread(send_ref[first : first + 1, :])
        low, high = index & (LANES - 1), index >> 7
        for tile in range(tiles):
            rows = slice(tile * 8, tile * 8 + 8)
            sources = [table_ref[rows, lanes(group)] for group in range(4)]
            pay_ref[rows, :] = pick(sources, low, high)


def start_kernel(near_ref, aggregates_ref, start_ref, sends_ref, table_ref, w_ref, send_ref, a_ref, b_ref):
    nodes = near_ref.shape[1]
    groups = nodes // 8
    for e in range(4):
        send_ref[e // 2 : e // 2 + 1, (e % 2) * 64 : (e % 2) * 64 + 64] = sends_ref[e : e + 1, :]
    name = lax.broadcasted_iota(jnp.int32, (groups, nodes), 0)
    members = (name == aggregates_ref[...]).astype(F32)
    sizes = jnp.sum(members, axis=1, keepdims=True)
    scale = lax.rsqrt(jnp.sum(members * sizes, axis=0, keepdims=True))
    table_ref[...] = jnp.zeros(table_ref.shape, F32)
    w_ref[...] = jnp.zeros(w_ref.shape, F32)
    for row in range(3):
        table_ref[row * 8 : row * 8 + 6, :] = near_ref[row * 6 : row * 6 + 6, :] * scale
        table_ref[row * 8 + 6 : row * 8 + 7, :] = start_ref[row : row + 1, :]
    w_ref[0:3, :] = start_ref[...]
    pack_rows(table_ref, 3, send_ref, (a_ref, b_ref))


def blocks_kernel(diag_ref, off_ref, columns_ref, scaled_ref, index_ref):
    slots = off_ref.shape[1]
    index_ref[0:slots, :] = columns_ref[...]
    index_ref[slots:, :] = jnp.zeros((index_ref.shape[0] - slots, index_ref.shape[1]), jnp.int32)
    scaled_ref[:, slots:, :] = jnp.zeros(
        (9, scaled_ref.shape[1] - slots, scaled_ref.shape[2]), F32
    )
    entries = [diag_ref[position : position + 1, :] for position in range(9)]
    cofactor = [
        entries[4] * entries[8] - entries[5] * entries[7],
        entries[5] * entries[6] - entries[3] * entries[8],
        entries[3] * entries[7] - entries[4] * entries[6],
        entries[2] * entries[7] - entries[1] * entries[8],
        entries[0] * entries[8] - entries[2] * entries[6],
        entries[1] * entries[6] - entries[0] * entries[7],
        entries[1] * entries[5] - entries[2] * entries[4],
        entries[2] * entries[3] - entries[0] * entries[5],
        entries[0] * entries[4] - entries[1] * entries[3],
    ]
    determinant = entries[0] * cofactor[0] + entries[1] * cofactor[1] + entries[2] * cofactor[2]
    inverse = [
        [cofactor[column * 3 + row] / determinant for column in range(3)] for row in range(3)
    ]
    for column in range(3):
        block = [off_ref[inner * 3 + column] for inner in range(3)]
        for row in range(3):
            total = inverse[row][0] * block[0]
            total = total + inverse[row][1] * block[1]
            total = total + inverse[row][2] * block[2]
            scaled_ref[row * 3 + column, 0:slots, :] = total


def ghost_row(refs, side_ref, axis, row):
    even, odd = refs
    use_odd = side_ref[axis : axis + 1, :] != 0
    return jnp.where(use_odd, odd[row : row + 1, :], even[row : row + 1, :])


def step_kernel(first, last, count, *refs):
    scaled_ref, index_ref, w_ref, ae, ao, be, bo, side_ref, send_ref = refs[:9]
    outs = refs[9:]
    next_ref = outs[0]
    table = []
    for c in range(3):
        row = c * 8 + 6 if first else c
        table.append(
            [spread(w_ref[c : c + 1, lanes(group)]) for group in range(4)]
            + [
                spread(ghost_row((ae, ao), side_ref, 0, row)),
                spread(ghost_row((be, bo), side_ref, 1, row)),
            ]
        )
    next_ref[...] = jnp.zeros(next_ref.shape, F32)
    for block in range(4):
        total = [None] * 3
        for tile in range(4):
            slots = slice(tile * 8, tile * 8 + 8)
            index = index_ref[slots, lanes(block)]
            low, high = index & (LANES - 1), index >> 7
            for c in range(3):
                found = pick(table[c], low, high)
                for r in range(3):
                    term = scaled_ref[r * 3 + c, slots, lanes(block)] * found
                    total[r] = term if total[r] is None else total[r] + term
        for r in range(3):
            next_ref[r : r + 1, lanes(block)] = w_ref[r : r + 1, lanes(block)] + jnp.sum(
                total[r], axis=0, keepdims=True
            )
    if last:
        sums_ref = outs[1]
        latest = jnp.sum(next_ref[...] * next_ref[...], keepdims=True)
        earlier = jnp.sum(w_ref[...] * w_ref[...], keepdims=True)
        lane = lax.broadcasted_iota(jnp.int32, (1, LANES), 1)
        both = jnp.where(lane == 0, latest, jnp.where(lane == 1, earlier, 0.0))
        sums_ref[...] = jnp.broadcast_to(both, (count, LANES))
    else:
        pack_rows(next_ref, 1, send_ref, outs[1:3])


def blocks_out_kernel(scaled_ref, index_ref, table_ref, ae, ao, be, bo, side_ref, out_ref):
    slots = out_ref.shape[1]
    use_odd = [side_ref[axis : axis + 1, :] != 0 for axis in range(2)]
    for block in range(4):
        for first in range(0, slots, 8):
            count = min(8, slots - first)
            tile = slice(first, first + 8)
            index = index_ref[tile, lanes(block)]
            low, high = index & (LANES - 1), index >> 7
            for m in range(6):
                found = []
                for c in range(3):
                    row = slice(c * 8 + m, c * 8 + m + 1)
                    sources = [spread(table_ref[row, lanes(group)]) for group in range(4)]
                    sources.append(spread(jnp.where(use_odd[0], ao[row, :], ae[row, :])))
                    sources.append(spread(jnp.where(use_odd[1], bo[row, :], be[row, :])))
                    found.append(pick(sources, low, high))
                for r in range(3):
                    total = None
                    for c in range(3):
                        term = scaled_ref[r * 3 + c, tile, lanes(block)] * found[c]
                        total = term if total is None else total + term
                    out_ref[r * 6 + m, first : first + count, lanes(block)] = total[0:count, :]


def regroup_kernel(sums_ref, out_ref):
    total = jnp.sum(sums_ref[...], axis=0, keepdims=True)
    out_ref[...] = jnp.broadcast_to(total, out_ref.shape)


def finish_kernel(sums_ref, raw_ref, table_ref, off_ref, self_ref, rho_ref):
    total = jnp.sum(sums_ref[...], axis=0, keepdims=True)
    lane = lax.broadcasted_iota(jnp.int32, (1, LANES), 1)
    latest = jnp.sum(jnp.where(lane == 0, total, 0.0), keepdims=True)
    earlier = jnp.sum(jnp.where(lane == 1, total, 0.0), keepdims=True)
    rho = jnp.sqrt(latest / (earlier + 1e-05))
    rho_ref[...] = jnp.broadcast_to(rho, rho_ref.shape)
    factor = -(OMEGA / rho)
    for entry in range(raw_ref.shape[0]):
        off_ref[entry] = (factor * raw_ref[entry]).astype(jnp.bfloat16)
    keep = 1.0 - OMEGA / rho
    for row in range(3):
        self_ref[row * 6 : row * 6 + 6, :] = (keep * table_ref[row * 8 : row * 8 + 6, :]).astype(
            jnp.bfloat16
        )


def call(kernel, name, outs, *args):
    return pl.pallas_call(
        kernel,
        name=name,
        out_shape=[
            jax.ShapeDtypeStruct(*out) if len(out) == 2 else pltpu.VMEM(*out[:2]) for out in outs
        ],
        in_specs=[VM] * len(args),
        out_specs=[VM] * len(outs),
        compiler_params=pltpu.CompilerParams(vmem_limit_bytes=16 << 20),
    )(*args)


def kept(array):
    return pltpu.with_memory_space_constraint(array, pltpu.VMEM)


def swap(count, offset):
    pairs = []
    for i in range(offset, count - 1, 2):
        pairs += [(i, i + 1), (i + 1, i)]
    return pairs


def exchange(a, b):
    subs, slabs = lax.axis_size(SUB), lax.axis_size("slab")
    ao = lax.ppermute(a, SUB, swap(subs, 1))
    be = lax.ppermute(b, "slab", swap(slabs, 0))
    bo = lax.ppermute(b, "slab", swap(slabs, 1))
    ae = lax.ppermute(a, SUB, swap(subs, 0))
    return ae, ao, be, bo


def body(near_null, aggregates, diag_block, off_blocks, columns, sends, start_vector):
    nodes = near_null.shape[1]
    slots = off_blocks.shape[0]
    padded = (slots + 7) // 8 * 8
    subs, slabs = lax.axis_size(SUB), lax.axis_size("slab")
    lane = jnp.arange(LANES, dtype=jnp.int32)[None, :]
    position = jnp.stack([lax.axis_index(SUB), lax.axis_index("slab")])[:, None] % 2
    side = ((lane < 64) == (position == 0)).astype(jnp.int32)

    kept_f32 = lambda *shape: (shape, F32, "kept")
    kept_i32 = lambda *shape: (shape, jnp.int32, "kept")
    table, w, send, a, b = call(
        start_kernel,
        "start",
        [kept_f32(24, nodes), kept_f32(8, nodes), kept_i32(2, LANES)]
        + [kept_f32(24, LANES)] * 2,
        near_null,
        aggregates[None, :],
        start_vector,
        sends,
    )
    received = [kept(x) for x in exchange(a, b)]
    side = kept(side)
    scaled, index = call(
        blocks_kernel,
        "blocks",
        [kept_f32(9, padded, nodes), kept_i32(padded, nodes)],
        diag_block,
        jnp.transpose(off_blocks, (1, 0, 2)),
        columns,
    )
    first_received = received
    for iteration in range(ITERS):
        last = iteration == ITERS - 1
        outs = [kept_f32(8, nodes)]
        outs += [kept_f32(subs, LANES)] if last else [kept_f32(8, LANES)] * 2
        result = call(
            functools.partial(step_kernel, iteration == 0, last, subs),
            f"step_{iteration}",
            outs,
            kept(scaled),
            kept(index),
            kept(w),
            *received,
            side,
            kept(send),
        )
        w = result[0]
        if last:
            sums = result[1]
        else:
            received = [kept(x) for x in exchange(result[1], result[2])]
    (raw,) = call(
        blocks_out_kernel,
        "blocks_out",
        [kept_f32(18, slots, nodes)],
        kept(scaled),
        kept(index),
        kept(table),
        *first_received,
        side,
    )
    sums = lax.all_to_all(sums, SUB, 0, 0, tiled=True)
    (sums,) = call(regroup_kernel, "regroup", [kept_f32(slabs, LANES)], kept(sums))
    sums = lax.all_to_all(sums, "slab", 0, 0, tiled=True)
    prolong_off, prolong_self, rho = call(
        finish_kernel,
        "finish",
        [((18, slots, nodes), jnp.bfloat16), ((18, nodes), jnp.bfloat16), ((1, LANES), F32)],
        kept(sums),
        kept(raw),
        kept(table),
    )
    return (jnp.transpose(prolong_off, (1, 0, 2)), prolong_self, rho[0, 0])


def solution(mesh):
    torus = Mesh(
        mesh.devices.reshape(mesh.shape["slab"], 8, 4, 2), ("slab", "sub_0", "sub_1", "sub_2")
    )
    placed = (
        P(None, SLAB_SUB),
        P(SLAB_SUB),
        P(None, SLAB_SUB),
        P(None, None, SLAB_SUB),
        P(None, SLAB_SUB),
        P(None, SLAB_SUB),
        P(None, SLAB_SUB),
    )
    return jax.shard_map(
        body,
        mesh=torus,
        in_specs=placed,
        out_specs=(P(None, None, SLAB_SUB), P(None, SLAB_SUB), P()),
        check_vma=False,
    )
```

profile of v0, /device:TPU:1, one launch (start us, length us, event | category | flops | bytes accessed | tf_op | source)
XLA Modules:
  0.0 171.8 jit_solution(1181436851889974015)
XLA Ops:
  3.7 4.5 %collective-permute-start.1 = (f32[24,128]{1,0:T(8,128)S(1)}, f32[24,128]{1,0:T(8,128)S(1)}, u32[]{:S(2)}, u32[]{:S(2)}) collective-permute-start(f32[24,128]{1,0:T(8,128)S(1)} %get-tuple-element.38), channel_id=1, source_target_pairs={{1,2},{2,1},{3,4},{4,3},{5,6},{6,5},{7,8},{8,7},{9,10},{10,9},{11,... | collective-permute-start | bytes 36872 | tf_op jit(solution)/shard_map/ppermute | solution.py:216
  8.2 8.5 %collective-permute-start = (f32[24,128]{1,0:T(8,128)S(1)}, f32[24,128]{1,0:T(8,128)S(1)}, u32[]{:S(2)}, u32[]{:S(2)}) collective-permute-start(f32[24,128]{1,0:T(8,128)S(1)} %get-tuple-element.38), channel_id=1, source_target_pairs={{0,1},{1,0},{2,3},{3,2},{4,5},{5,4},{6,7},{7,6},{8,9},{9,8},{10,11... | collective-permute-start | bytes 36872 | tf_op jit(solution)/shard_map/ppermute | solution.py:219
  17.4 1.9 %collective-permute-start.2 = (f32[24,128]{1,0:T(8,128)S(1)}, f32[24,128]{1,0:T(8,128)S(1)}, u32[]{:S(2)}, u32[]{:S(2)}) collective-permute-start(f32[24,128]{1,0:T(8,128)S(1)} %get-tuple-element.39), channel_id=1, source_target_pairs={{0,64},{64,0},{128,192},{192,128},{256,320},{320,256},{384,448},{4... | collective-permute-start | bytes 36872 | tf_op jit(solution)/shard_map/ppermute | solution.py:217
  22.9 2.8 %collective-permute-start.5 = (f32[8,128]{1,0:T(8,128)S(1)}, f32[8,128]{1,0:T(8,128)S(1)}, u32[]{:S(2)}, u32[]{:S(2)}) collective-permute-start(f32[8,128]{1,0:T(8,128)S(1)} %get-tuple-element.42), channel_id=1, source_target_pairs={{1,2},{2,1},{3,4},{4,3},{5,6},{6,5},{7,8},{8,7},{9,10},{10,9},{11,... | collective-permute-start | bytes 12296 | tf_op jit(solution)/shard_map/ppermute | solution.py:216
  25.8 1.9 %collective-permute-start.4 = (f32[8,128]{1,0:T(8,128)S(1)}, f32[8,128]{1,0:T(8,128)S(1)}, u32[]{:S(2)}, u32[]{:S(2)}) collective-permute-start(f32[8,128]{1,0:T(8,128)S(1)} %get-tuple-element.42), channel_id=1, source_target_pairs={{0,1},{1,0},{2,3},{3,2},{4,5},{5,4},{6,7},{7,6},{8,9},{9,8},{10,11... | collective-permute-start | bytes 12296 | tf_op jit(solution)/shard_map/ppermute | solution.py:219
  28.4 8.6 %collective-permute-start.6 = (f32[8,128]{1,0:T(8,128)S(1)}, f32[8,128]{1,0:T(8,128)S(1)}, u32[]{:S(2)}, u32[]{:S(2)}) collective-permute-start(f32[8,128]{1,0:T(8,128)S(1)} %get-tuple-element.43), channel_id=1, source_target_pairs={{0,64},{64,0},{128,192},{192,128},{256,320},{320,256},{384,448},{4... | collective-permute-start | bytes 12296 | tf_op jit(solution)/shard_map/ppermute | solution.py:217
  38.4 4.4 %collective-permute-start.9 = (f32[8,128]{1,0:T(8,128)S(1)}, f32[8,128]{1,0:T(8,128)S(1)}, u32[]{:S(2)}, u32[]{:S(2)}) collective-permute-start(f32[8,128]{1,0:T(8,128)S(1)} %get-tuple-element.45), channel_id=1, source_target_pairs={{1,2},{2,1},{3,4},{4,3},{5,6},{6,5},{7,8},{8,7},{9,10},{10,9},{11,... | collective-permute-start | bytes 12296 | tf_op jit(solution)/shard_map/ppermute | solution.py:216
  42.8 1.9 %collective-permute-start.8 = (f32[8,128]{1,0:T(8,128)S(1)}, f32[8,128]{1,0:T(8,128)S(1)}, u32[]{:S(2)}, u32[]{:S(2)}) collective-permute-start(f32[8,128]{1,0:T(8,128)S(1)} %get-tuple-element.45), channel_id=1, source_target_pairs={{0,1},{1,0},{2,3},{3,2},{4,5},{5,4},{6,7},{7,6},{8,9},{9,8},{10,11... | collective-permute-start | bytes 12296 | tf_op jit(solution)/shard_map/ppermute | solution.py:219
  45.4 7.3 %collective-permute-start.10 = (f32[8,128]{1,0:T(8,128)S(1)}, f32[8,128]{1,0:T(8,128)S(1)}, u32[]{:S(2)}, u32[]{:S(2)}) collective-permute-start(f32[8,128]{1,0:T(8,128)S(1)} %get-tuple-element.46), channel_id=1, source_target_pairs={{0,64},{64,0},{128,192},{192,128},{256,320},{320,256},{384,448},{4... | collective-permute-start | bytes 12296 | tf_op jit(solution)/shard_map/ppermute | solution.py:217
  54.2 4.6 %collective-permute-start.13 = (f32[8,128]{1,0:T(8,128)S(1)}, f32[8,128]{1,0:T(8,128)S(1)}, u32[]{:S(2)}, u32[]{:S(2)}) collective-permute-start(f32[8,128]{1,0:T(8,128)S(1)} %get-tuple-element.48), channel_id=1, source_target_pairs={{1,2},{2,1},{3,4},{4,3},{5,6},{6,5},{7,8},{8,7},{9,10},{10,9},{11,... | collective-permute-start | bytes 12296 | tf_op jit(solution)/shard_map/ppermute | solution.py:216
  58.9 1.9 %collective-permute-start.12 = (f32[8,128]{1,0:T(8,128)S(1)}, f32[8,128]{1,0:T(8,128)S(1)}, u32[]{:S(2)}, u32[]{:S(2)}) collective-permute-start(f32[8,128]{1,0:T(8,128)S(1)} %get-tuple-element.48), channel_id=1, source_target_pairs={{0,1},{1,0},{2,3},{3,2},{4,5},{5,4},{6,7},{7,6},{8,9},{9,8},{10,11... | collective-permute-start | bytes 12296 | tf_op jit(solution)/shard_map/ppermute | solution.py:219
  61.5 6.1 %collective-permute-start.14 = (f32[8,128]{1,0:T(8,128)S(1)}, f32[8,128]{1,0:T(8,128)S(1)}, u32[]{:S(2)}, u32[]{:S(2)}) collective-permute-start(f32[8,128]{1,0:T(8,128)S(1)} %get-tuple-element.49), channel_id=1, source_target_pairs={{0,64},{64,0},{128,192},{192,128},{256,320},{320,256},{384,448},{4... | collective-permute-start | bytes 12296 | tf_op jit(solution)/shard_map/ppermute | solution.py:217
  69.1 5.1 %collective-permute-start.17 = (f32[8,128]{1,0:T(8,128)S(1)}, f32[8,128]{1,0:T(8,128)S(1)}, u32[]{:S(2)}, u32[]{:S(2)}) collective-permute-start(f32[8,128]{1,0:T(8,128)S(1)} %get-tuple-element.51), channel_id=1, source_target_pairs={{1,2},{2,1},{3,4},{4,3},{5,6},{6,5},{7,8},{8,7},{9,10},{10,9},{11,... | collective-permute-start | bytes 12296 | tf_op jit(solution)/shard_map/ppermute | solution.py:216
  76.9 6.3 %collective-permute-start.18 = (f32[8,128]{1,0:T(8,128)S(1)}, f32[8,128]{1,0:T(8,128)S(1)}, u32[]{:S(2)}, u32[]{:S(2)}) collective-permute-start(f32[8,128]{1,0:T(8,128)S(1)} %get-tuple-element.52), channel_id=1, source_target_pairs={{0,64},{64,0},{128,192},{192,128},{256,320},{320,256},{384,448},{4... | collective-permute-start | bytes 12296 | tf_op jit(solution)/shard_map/ppermute | solution.py:217
  84.7 4.3 %collective-permute-start.21 = (f32[8,128]{1,0:T(8,128)S(1)}, f32[8,128]{1,0:T(8,128)S(1)}, u32[]{:S(2)}, u32[]{:S(2)}) collective-permute-start(f32[8,128]{1,0:T(8,128)S(1)} %get-tuple-element.54), channel_id=1, source_target_pairs={{1,2},{2,1},{3,4},{4,3},{5,6},{6,5},{7,8},{8,7},{9,10},{10,9},{11,... | collective-permute-start | bytes 12296 | tf_op jit(solution)/shard_map/ppermute | solution.py:216
  91.5 6.1 %collective-permute-start.22 = (f32[8,128]{1,0:T(8,128)S(1)}, f32[8,128]{1,0:T(8,128)S(1)}, u32[]{:S(2)}, u32[]{:S(2)}) collective-permute-start(f32[8,128]{1,0:T(8,128)S(1)} %get-tuple-element.55), channel_id=1, source_target_pairs={{0,64},{64,0},{128,192},{192,128},{256,320},{320,256},{384,448},{4... | collective-permute-start | bytes 12296 | tf_op jit(solution)/shard_map/ppermute | solution.py:217
  99.2 4.5 %collective-permute-start.25 = (f32[8,128]{1,0:T(8,128)S(1)}, f32[8,128]{1,0:T(8,128)S(1)}, u32[]{:S(2)}, u32[]{:S(2)}) collective-permute-start(f32[8,128]{1,0:T(8,128)S(1)} %get-tuple-element.57), channel_id=1, source_target_pairs={{1,2},{2,1},{3,4},{4,3},{5,6},{6,5},{7,8},{8,7},{9,10},{10,9},{11,... | collective-permute-start | bytes 12296 | tf_op jit(solution)/shard_map/ppermute | solution.py:216
  106.3 6.0 %collective-permute-start.26 = (f32[8,128]{1,0:T(8,128)S(1)}, f32[8,128]{1,0:T(8,128)S(1)}, u32[]{:S(2)}, u32[]{:S(2)}) collective-permute-start(f32[8,128]{1,0:T(8,128)S(1)} %get-tuple-element.58), channel_id=1, source_target_pairs={{0,64},{64,0},{128,192},{192,128},{256,320},{320,256},{384,448},{4... | collective-permute-start | bytes 12296 | tf_op jit(solution)/shard_map/ppermute | solution.py:217
  113.8 4.6 %collective-permute-start.29 = (f32[8,128]{1,0:T(8,128)S(1)}, f32[8,128]{1,0:T(8,128)S(1)}, u32[]{:S(2)}, u32[]{:S(2)}) collective-permute-start(f32[8,128]{1,0:T(8,128)S(1)} %get-tuple-element.60), channel_id=1, source_target_pairs={{1,2},{2,1},{3,4},{4,3},{5,6},{6,5},{7,8},{8,7},{9,10},{10,9},{11,... | collective-permute-start | bytes 12296 | tf_op jit(solution)/shard_map/ppermute | solution.py:216
  121.1 6.1 %collective-permute-start.30 = (f32[8,128]{1,0:T(8,128)S(1)}, f32[8,128]{1,0:T(8,128)S(1)}, u32[]{:S(2)}, u32[]{:S(2)}) collective-permute-start(f32[8,128]{1,0:T(8,128)S(1)} %get-tuple-element.61), channel_id=1, source_target_pairs={{0,64},{64,0},{128,192},{192,128},{256,320},{320,256},{384,448},{4... | collective-permute-start | bytes 12296 | tf_op jit(solution)/shard_map/ppermute | solution.py:217
  129.3 22.5 %all_to_all.22 = f32[64,1,128]{2,1,0:T(1,128)S(1)} all-to-all(f32[64,1,128]{2,1,0:T(1,128)S(1)} %bitcast.19), channel_id=1, replica_groups=mesh['slab'=12,'sub_0'=8,'sub_1'=4,'sub_2'=2] {'sub_0','sub_1','sub_2'}, dimensions={0} | all-to-all | bytes 65536 | tf_op jit(solution)/shard_map/all_to_all | solution.py:285
  152.3 9.6 %all-to-all-start.1 = ((f32[12,1,128]{2,1,0:T(1,128)}), f32[12,1,128]{2,1,0:T(1,128)S(1)}, u32[]{:S(2)}, u32[]{:S(2)}) async-start(f32[12,1,128]{2,1,0:T(1,128)} %copy.11), calls=%async_computation.1 | async-start | bytes 12288 | tf_op jit(solution)/shard_map/all_to_all | solution.py:287
  161.9 2.0 %blocks_out.1.raw_ref = f32[18,26,512]{2,1,0:T(8,128)S(1)} custom-call(f32[9,32,512]{2,1,0:T(8,128)S(1)} %get-tuple-element.35.refs_0_.scaled_ref, s32[32,512]{1,0:T(8,128)S(1)} %get-tuple-element.36.refs_1_.index_ref, f32[24,512]{1,0:T(8,128)S(1)} %get-tuple-element.63.table_ref, f32[24,128]{1,0:T(8,128)S(1)} %collective-permute-done.refs_3_.ae, ...), custom_call_target="tpu_custom_call" | custom-call | tf_op jit(solution)/shard_map/blocks_out/pallas_call | solution.py:191
  163.9 6.9 %all-to-all-done.1 = f32[12,1,128]{2,1,0:T(1,128)S(1)} async-done(((f32[12,1,128]{2,1,0:T(1,128)}), f32[12,1,128]{2,1,0:T(1,128)S(1)}, u32[]{:S(2)}, u32[]{:S(2)}) %all-to-all-start.1) | async-done | bytes 6176 | tf_op jit(solution)/shard_map/all_to_all | solution.py:287
  (75 shorter events, 32.0 us)
Async XLA Ops:
  3.7 18.7 %collective-permute-start.1 = (f32[24,128]{1,0:T(8,128)S(1)}, f32[24,128]{1,0:T(8,128)S(1)}, u32[]{:S(2)}, u32[]{:S(2)}) collective-permute-start(f32[24,128]{1,0:T(8,128)S(1)} %get-tuple-element.38), channel_id=1, source_target_pairs={{1,2},{2,1},{3,4},{4,3},{5,6},{6,5},{7,8},{8,7},{9,10},{10,9},{11,... | collective-permute-start | bytes 36872 | tf_op jit(solution)/shard_map/ppermute | solution.py:216
  8.2 14.2 %collective-permute-start = (f32[24,128]{1,0:T(8,128)S(1)}, f32[24,128]{1,0:T(8,128)S(1)}, u32[]{:S(2)}, u32[]{:S(2)}) collective-permute-start(f32[24,128]{1,0:T(8,128)S(1)} %get-tuple-element.38), channel_id=1, source_target_pairs={{0,1},{1,0},{2,3},{3,2},{4,5},{5,4},{6,7},{7,6},{8,9},{9,8},{10,11... | collective-permute-start | bytes 36872 | tf_op jit(solution)/shard_map/ppermute | solution.py:219
  22.9 14.0 %collective-permute-start.5 = (f32[8,128]{1,0:T(8,128)S(1)}, f32[8,128]{1,0:T(8,128)S(1)}, u32[]{:S(2)}, u32[]{:S(2)}) collective-permute-start(f32[8,128]{1,0:T(8,128)S(1)} %get-tuple-element.42), channel_id=1, source_target_pairs={{1,2},{2,1},{3,4},{4,3},{5,6},{6,5},{7,8},{8,7},{9,10},{10,9},{11,... | collective-permute-start | bytes 12296 | tf_op jit(solution)/shard_map/ppermute | solution.py:216
  25.8 11.2 %collective-permute-start.4 = (f32[8,128]{1,0:T(8,128)S(1)}, f32[8,128]{1,0:T(8,128)S(1)}, u32[]{:S(2)}, u32[]{:S(2)}) collective-permute-start(f32[8,128]{1,0:T(8,128)S(1)} %get-tuple-element.42), channel_id=1, source_target_pairs={{0,1},{1,0},{2,3},{3,2},{4,5},{5,4},{6,7},{7,6},{8,9},{9,8},{10,11... | collective-permute-start | bytes 12296 | tf_op jit(solution)/shard_map/ppermute | solution.py:219
  27.7 9.3 %collective-permute-start.7 = (f32[8,128]{1,0:T(8,128)S(1)}, f32[8,128]{1,0:T(8,128)S(1)}, u32[]{:S(2)}, u32[]{:S(2)}) collective-permute-start(f32[8,128]{1,0:T(8,128)S(1)} %get-tuple-element.43), channel_id=1, source_target_pairs={{64,128},{128,64},{192,256},{256,192},{320,384},{384,320},{448,512... | collective-permute-start | bytes 12296 | tf_op jit(solution)/shard_map/ppermute | solution.py:218
  28.4 9.5 %collective-permute-start.6 = (f32[8,128]{1,0:T(8,128)S(1)}, f32[8,128]{1,0:T(8,128)S(1)}, u32[]{:S(2)}, u32[]{:S(2)}) collective-permute-start(f32[8,128]{1,0:T(8,128)S(1)} %get-tuple-element.43), channel_id=1, source_target_pairs={{0,64},{64,0},{128,192},{192,128},{256,320},{320,256},{384,448},{4... | collective-permute-start | bytes 12296 | tf_op jit(solution)/shard_map/ppermute | solution.py:217
  38.4 14.3 %collective-permute-start.9 = (f32[8,128]{1,0:T(8,128)S(1)}, f32[8,128]{1,0:T(8,128)S(1)}, u32[]{:S(2)}, u32[]{:S(2)}) collective-permute-start(f32[8,128]{1,0:T(8,128)S(1)} %get-tuple-element.45), channel_id=1, source_target_pairs={{1,2},{2,1},{3,4},{4,3},{5,6},{6,5},{7,8},{8,7},{9,10},{10,9},{11,... | collective-permute-start | bytes 12296 | tf_op jit(solution)/shard_map/ppermute | solution.py:216
  42.8 10.0 %collective-permute-start.8 = (f32[8,128]{1,0:T(8,128)S(1)}, f32[8,128]{1,0:T(8,128)S(1)}, u32[]{:S(2)}, u32[]{:S(2)}) collective-permute-start(f32[8,128]{1,0:T(8,128)S(1)} %get-tuple-element.45), channel_id=1, source_target_pairs={{0,1},{1,0},{2,3},{3,2},{4,5},{5,4},{6,7},{7,6},{8,9},{9,8},{10,11... | collective-permute-start | bytes 12296 | tf_op jit(solution)/shard_map/ppermute | solution.py:219
  44.7 8.0 %collective-permute-start.11 = (f32[8,128]{1,0:T(8,128)S(1)}, f32[8,128]{1,0:T(8,128)S(1)}, u32[]{:S(2)}, u32[]{:S(2)}) collective-permute-start(f32[8,128]{1,0:T(8,128)S(1)} %get-tuple-element.46), channel_id=1, source_target_pairs={{64,128},{128,64},{192,256},{256,192},{320,384},{384,320},{448,512... | collective-permute-start | bytes 12296 | tf_op jit(solution)/shard_map/ppermute | solution.py:218
  45.4 8.3 %collective-permute-start.10 = (f32[8,128]{1,0:T(8,128)S(1)}, f32[8,128]{1,0:T(8,128)S(1)}, u32[]{:S(2)}, u32[]{:S(2)}) collective-permute-start(f32[8,128]{1,0:T(8,128)S(1)} %get-tuple-element.46), channel_id=1, source_target_pairs={{0,64},{64,0},{128,192},{192,128},{256,320},{320,256},{384,448},{4... | collective-permute-start | bytes 12296 | tf_op jit(solution)/shard_map/ppermute | solution.py:217
  54.2 13.4 %collective-permute-start.13 = (f32[8,128]{1,0:T(8,128)S(1)}, f32[8,128]{1,0:T(8,128)S(1)}, u32[]{:S(2)}, u32[]{:S(2)}) collective-permute-start(f32[8,128]{1,0:T(8,128)S(1)} %get-tuple-element.48), channel_id=1, source_target_pairs={{1,2},{2,1},{3,4},{4,3},{5,6},{6,5},{7,8},{8,7},{9,10},{10,9},{11,... | collective-permute-start | bytes 12296 | tf_op jit(solution)/shard_map/ppermute | solution.py:216
  58.9 8.8 %collective-permute-start.12 = (f32[8,128]{1,0:T(8,128)S(1)}, f32[8,128]{1,0:T(8,128)S(1)}, u32[]{:S(2)}, u32[]{:S(2)}) collective-permute-start(f32[8,128]{1,0:T(8,128)S(1)} %get-tuple-element.48), channel_id=1, source_target_pairs={{0,1},{1,0},{2,3},{3,2},{4,5},{5,4},{6,7},{7,6},{8,9},{9,8},{10,11... | collective-permute-start | bytes 12296 | tf_op jit(solution)/shard_map/ppermute | solution.py:219
  61.5 7.1 %collective-permute-start.14 = (f32[8,128]{1,0:T(8,128)S(1)}, f32[8,128]{1,0:T(8,128)S(1)}, u32[]{:S(2)}, u32[]{:S(2)}) collective-permute-start(f32[8,128]{1,0:T(8,128)S(1)} %get-tuple-element.49), channel_id=1, source_target_pairs={{0,64},{64,0},{128,192},{192,128},{256,320},{320,256},{384,448},{4... | collective-permute-start | bytes 12296 | tf_op jit(solution)/shard_map/ppermute | solution.py:217
  69.1 14.1 %collective-permute-start.17 = (f32[8,128]{1,0:T(8,128)S(1)}, f32[8,128]{1,0:T(8,128)S(1)}, u32[]{:S(2)}, u32[]{:S(2)}) collective-permute-start(f32[8,128]{1,0:T(8,128)S(1)} %get-tuple-element.51), channel_id=1, source_target_pairs={{1,2},{2,1},{3,4},{4,3},{5,6},{6,5},{7,8},{8,7},{9,10},{10,9},{11,... | collective-permute-start | bytes 12296 | tf_op jit(solution)/shard_map/ppermute | solution.py:216
  74.3 8.9 %collective-permute-start.16 = (f32[8,128]{1,0:T(8,128)S(1)}, f32[8,128]{1,0:T(8,128)S(1)}, u32[]{:S(2)}, u32[]{:S(2)}) collective-permute-start(f32[8,128]{1,0:T(8,128)S(1)} %get-tuple-element.51), channel_id=1, source_target_pairs={{0,1},{1,0},{2,3},{3,2},{4,5},{5,4},{6,7},{7,6},{8,9},{9,8},{10,11... | collective-permute-start | bytes 12296 | tf_op jit(solution)/shard_map/ppermute | solution.py:219
  76.9 7.3 %collective-permute-start.18 = (f32[8,128]{1,0:T(8,128)S(1)}, f32[8,128]{1,0:T(8,128)S(1)}, u32[]{:S(2)}, u32[]{:S(2)}) collective-permute-start(f32[8,128]{1,0:T(8,128)S(1)} %get-tuple-element.52), channel_id=1, source_target_pairs={{0,64},{64,0},{128,192},{192,128},{256,320},{320,256},{384,448},{4... | collective-permute-start | bytes 12296 | tf_op jit(solution)/shard_map/ppermute | solution.py:217
  84.7 13.0 %collective-permute-start.21 = (f32[8,128]{1,0:T(8,128)S(1)}, f32[8,128]{1,0:T(8,128)S(1)}, u32[]{:S(2)}, u32[]{:S(2)}) collective-permute-start(f32[8,128]{1,0:T(8,128)S(1)} %get-tuple-element.54), channel_id=1, source_target_pairs={{1,2},{2,1},{3,4},{4,3},{5,6},{6,5},{7,8},{8,7},{9,10},{10,9},{11,... | collective-permute-start | bytes 12296 | tf_op jit(solution)/shard_map/ppermute | solution.py:216
  88.9 8.8 %collective-permute-start.20 = (f32[8,128]{1,0:T(8,128)S(1)}, f32[8,128]{1,0:T(8,128)S(1)}, u32[]{:S(2)}, u32[]{:S(2)}) collective-permute-start(f32[8,128]{1,0:T(8,128)S(1)} %get-tuple-element.54), channel_id=1, source_target_pairs={{0,1},{1,0},{2,3},{3,2},{4,5},{5,4},{6,7},{7,6},{8,9},{9,8},{10,11... | collective-permute-start | bytes 12296 | tf_op jit(solution)/shard_map/ppermute | solution.py:219
  91.5 7.1 %collective-permute-start.22 = (f32[8,128]{1,0:T(8,128)S(1)}, f32[8,128]{1,0:T(8,128)S(1)}, u32[]{:S(2)}, u32[]{:S(2)}) collective-permute-start(f32[8,128]{1,0:T(8,128)S(1)} %get-tuple-element.55), channel_id=1, source_target_pairs={{0,64},{64,0},{128,192},{192,128},{256,320},{320,256},{384,448},{4... | collective-permute-start | bytes 12296 | tf_op jit(solution)/shard_map/ppermute | solution.py:217
  99.2 13.2 %collective-permute-start.25 = (f32[8,128]{1,0:T(8,128)S(1)}, f32[8,128]{1,0:T(8,128)S(1)}, u32[]{:S(2)}, u32[]{:S(2)}) collective-permute-start(f32[8,128]{1,0:T(8,128)S(1)} %get-tuple-element.57), channel_id=1, source_target_pairs={{1,2},{2,1},{3,4},{4,3},{5,6},{6,5},{7,8},{8,7},{9,10},{10,9},{11,... | collective-permute-start | bytes 12296 | tf_op jit(solution)/shard_map/ppermute | solution.py:216
  103.7 8.6 %collective-permute-start.24 = (f32[8,128]{1,0:T(8,128)S(1)}, f32[8,128]{1,0:T(8,128)S(1)}, u32[]{:S(2)}, u32[]{:S(2)}) collective-permute-start(f32[8,128]{1,0:T(8,128)S(1)} %get-tuple-element.57), channel_id=1, source_target_pairs={{0,1},{1,0},{2,3},{3,2},{4,5},{5,4},{6,7},{7,6},{8,9},{9,8},{10,11... | collective-permute-start | bytes 12296 | tf_op jit(solution)/shard_map/ppermute | solution.py:219
  113.8 13.4 %collective-permute-start.29 = (f32[8,128]{1,0:T(8,128)S(1)}, f32[8,128]{1,0:T(8,128)S(1)}, u32[]{:S(2)}, u32[]{:S(2)}) collective-permute-start(f32[8,128]{1,0:T(8,128)S(1)} %get-tuple-element.60), channel_id=1, source_target_pairs={{1,2},{2,1},{3,4},{4,3},{5,6},{6,5},{7,8},{8,7},{9,10},{10,9},{11,... | collective-permute-start | bytes 12296 | tf_op jit(solution)/shard_map/ppermute | solution.py:216
  118.5 8.8 %collective-permute-start.28 = (f32[8,128]{1,0:T(8,128)S(1)}, f32[8,128]{1,0:T(8,128)S(1)}, u32[]{:S(2)}, u32[]{:S(2)}) collective-permute-start(f32[8,128]{1,0:T(8,128)S(1)} %get-tuple-element.60), channel_id=1, source_target_pairs={{0,1},{1,0},{2,3},{3,2},{4,5},{5,4},{6,7},{7,6},{8,9},{9,8},{10,11... | collective-permute-start | bytes 12296 | tf_op jit(solution)/shard_map/ppermute | solution.py:219
  152.3 18.5 %all-to-all-start.1 = ((f32[12,1,128]{2,1,0:T(1,128)}), f32[12,1,128]{2,1,0:T(1,128)S(1)}, u32[]{:S(2)}, u32[]{:S(2)}) async-start(f32[12,1,128]{2,1,0:T(1,128)} %copy.11), calls=%async_computation.1 | async-start | bytes 12288 | tf_op jit(solution)/shard_map/all_to_all | solution.py:287
  (16 other events, 64.5 us)
where the time goes:
time: 173 us; the launch traced here: 172 us
  starting transfers between devices  120 us (69%)
  blocking collectives  22.5 us (13%)
  waiting for transfers between devices  13.6 us (8%)
  Pallas kernels  7.97 us (5%)
  local copies, waits for them, and re-layouts  6.12 us (4%)
    ppermute x8, starting transfers between devices, exchange(): be = lax.ppermute(b, 'slab', swap(slabs, 0))  48.6 us
    ppermute x8, starting transfers between devices, exchange(): ao = lax.ppermute(a, SUB, swap(subs, 1))  34.9 us
    all_to_all x1, blocking collectives, body(): sums = lax.all_to_all(sums, SUB, 0, 0, tiled=True)  22.5 us
    ppermute x8, starting transfers between devices, exchange(): ae = lax.ppermute(a, SUB, swap(subs, 0))  22 us
    all_to_all x1, starting transfers between devices, body(): sums = lax.all_to_all(sums, 'slab', 0, 0, tiled=True)  9.58 us
    pallas_call x13, Pallas kernels, call(): pl.pallas_call(kernel, name=name, out_shape=[jax.ShapeDtypeStruct(*out) i...  7.97 us
    all_to_all x1, waiting for transfers between devices, body(): sums = lax.all_to_all(sums, 'slab', 0, 0, tiled=True)  6.88 us
    ppermute x8, waiting for transfers between devices, exchange(): be = lax.ppermute(b, 'slab', swap(slabs, 0))  6.65 us
  transfers between devices with their start and end apart: 33, of which 8 were waited for; matrix products, arithmetic and copies ran while one was open for 0% of the time, Pallas kernels for 1%

commit v1 on v0

--- a/solution.py
+++ b/solution.py
@@ -14,6 +14,8 @@
 SLAB_SUB = ("slab", "sub_0", "sub_1", "sub_2")
 LANES = 128
 F32 = jnp.float32
+MODE = "square"
+RECEIVED = {"perm": 4, "core": 4, "square": 3}[MODE]
 VM = pl.BlockSpec(memory_space=pltpu.VMEM)
 
 
@@ -33,7 +35,7 @@
     return jnp.broadcast_to(row, (8, LANES))
 
 
-def pack_rows(table_ref, tiles, send_ref, pay_refs):
+def pack_rows(table_ref, tiles, send_ref, pay_refs, both_ref):
     for pay_ref, first in zip(pay_refs, (0, 1)):
         index = spread(send_ref[first : first + 1, :])
         low, high = index & (LANES - 1), index >> 7
@@ -41,9 +43,11 @@
             rows = slice(tile * 8, tile * 8 + 8)
             sources = [table_ref[rows, lanes(group)] for group in range(4)]
             pay_ref[rows, :] = pick(sources, low, high)
-
-
-def start_kernel(near_ref, aggregates_ref, start_ref, sends_ref, table_ref, w_ref, send_ref, a_ref, b_ref):
+    both_ref[0 : tiles * 8, :] = pay_refs[0][...]
+    both_ref[tiles * 8 :, :] = pay_refs[1][...]
+
+
+def start_kernel(near_ref, aggregates_ref, start_ref, sends_ref, table_ref, w_ref, send_ref, a_ref, b_ref, both_ref):
     nodes = near_ref.shape[1]
     groups = nodes // 8
     for e in range(4):
@@ -58,7 +62,7 @@
         table_ref[row * 8 : row * 8 + 6, :] = near_ref[row * 6 : row * 6 + 6, :] * scale
         table_ref[row * 8 + 6 : row * 8 + 7, :] = start_ref[row : row + 1, :]
     w_ref[0:3, :] = start_ref[...]
-    pack_rows(table_ref, 3, send_ref, (a_ref, b_ref))
+    pack_rows(table_ref, 3, send_ref, (a_ref, b_ref), both_ref)
 
 
 def blocks_kernel(diag_ref, off_ref, columns_ref, scaled_ref, index_ref):
@@ -93,25 +97,51 @@
             scaled_ref[row * 3 + column, 0:slots, :] = total
 
 
-def ghost_row(refs, side_ref, axis, row):
-    even, odd = refs
-    use_odd = side_ref[axis : axis + 1, :] != 0
-    return jnp.where(use_odd, odd[row : row + 1, :], even[row : row + 1, :])
+def ghost_rows(refs, side_ref, row):
+    if MODE == "perm":
+        ae, ao, be, bo = refs
+        even = ae[row, :], be[row, :]
+        odd = ao[row, :], bo[row, :]
+    elif MODE == "core":
+        ao, be, bo, gathered = refs
+        odd_sub = side_ref[2:3, :] != 0
+        even = jnp.where(odd_sub, gathered[0, row, :], gathered[1, row, :]), be[row, :]
+        odd = ao[row, :], bo[row, :]
+    else:
+        ao, bo, gathered = refs
+        odd_sub = side_ref[2:3, :] != 0
+        odd_slab = side_ref[3:4, :] != 0
+        half = gathered.shape[1] // 2
+        down = slice(row.start + half, row.stop + half)
+        even_a = jnp.where(
+            odd_slab,
+            jnp.where(odd_sub, gathered[2, row, :], gathered[3, row, :]),
+            jnp.where(odd_sub, gathered[0, row, :], gathered[1, row, :]),
+        )
+        even_b = jnp.where(
+            odd_slab,
+            jnp.where(odd_sub, gathered[1, down, :], gathered[0, down, :]),
+            jnp.where(odd_sub, gathered[3, down, :], gathered[2, down, :]),
+        )
+        even = even_a, even_b
+        odd = ao[row, :], bo[row, :]
+    return [
+        spread(jnp.where(side_ref[axis : axis + 1, :] != 0, odd[axis], even[axis]))
+        for axis in range(2)
+    ]
 
 
 def step_kernel(first, last, count, *refs):
-    scaled_ref, index_ref, w_ref, ae, ao, be, bo, side_ref, send_ref = refs[:9]
-    outs = refs[9:]
+    scaled_ref, index_ref, w_ref, side_ref, send_ref = refs[:5]
+    received = refs[5 : 5 + RECEIVED]
+    outs = refs[5 + RECEIVED :]
     next_ref = outs[0]
     table = []
     for c in range(3):
         row = c * 8 + 6 if first else c
         table.append(
             [spread(w_ref[c : c + 1, lanes(group)]) for group in range(4)]
-            + [
-                spread(ghost_row((ae, ao), side_ref, 0, row)),
-                spread(ghost_row((be, bo), side_ref, 1, row)),
-            ]
+            + ghost_rows(received, side_ref, slice(row, row + 1))
         )
     next_ref[...] = jnp.zeros(next_ref.shape, F32)
     for block in range(4):
@@ -135,14 +165,14 @@
         earlier = jnp.sum(w_ref[...] * w_ref[...], keepdims=True)
         lane = lax.broadcasted_iota(jnp.int32, (1, LANES), 1)
         both = jnp.where(lane == 0, latest, jnp.where(lane == 1, earlier, 0.0))
-        sums_ref[...] = jnp.broadcast_to(both, (count, LANES))
+        sums_ref[...] = jnp.broadcast_to(both[None], (count, 1, LANES))
     else:
-        pack_rows(next_ref, 1, send_ref, outs[1:3])
-
-
-def blocks_out_kernel(scaled_ref, index_ref, table_ref, ae, ao, be, bo, side_ref, out_ref):
+        pack_rows(next_ref, 1, send_ref, outs[1:3], outs[3])
+
+
+def blocks_out_kernel(scaled_ref, index_ref, table_ref, side_ref, *refs):
+    received, out_ref = refs[:RECEIVED], refs[RECEIVED]
     slots = out_ref.shape[1]
-    use_odd = [side_ref[axis : axis + 1, :] != 0 for axis in range(2)]
     for block in range(4):
         for first in range(0, slots, 8):
             count = min(8, slots - first)
@@ -154,9 +184,7 @@
                 for c in range(3):
                     row = slice(c * 8 + m, c * 8 + m + 1)
                     sources = [spread(table_ref[row, lanes(group)]) for group in range(4)]
-                    sources.append(spread(jnp.where(use_odd[0], ao[row, :], ae[row, :])))
-                    sources.append(spread(jnp.where(use_odd[1], bo[row, :], be[row, :])))
-                    found.append(pick(sources, low, high))
+                    found.append(pick(sources + ghost_rows(received, side_ref, row), low, high))
                 for r in range(3):
                     total = None
                     for c in range(3):
@@ -171,7 +199,7 @@
 
 
 def finish_kernel(sums_ref, raw_ref, table_ref, off_ref, self_ref, rho_ref):
-    total = jnp.sum(sums_ref[...], axis=0, keepdims=True)
+    total = jnp.sum(sums_ref[...], axis=0)
     lane = lax.broadcasted_iota(jnp.int32, (1, LANES), 1)
     latest = jnp.sum(jnp.where(lane == 0, total, 0.0), keepdims=True)
     earlier = jnp.sum(jnp.where(lane == 1, total, 0.0), keepdims=True)
@@ -187,10 +215,9 @@
         )
 
 
-def call(kernel, name, outs, *args):
+def call(kernel, outs, *args):
     return pl.pallas_call(
         kernel,
-        name=name,
         out_shape=[
             jax.ShapeDtypeStruct(*out) if len(out) == 2 else pltpu.VMEM(*out[:2]) for out in outs
         ],
@@ -200,6 +227,10 @@
     )(*args)
 
 
+def far(array):
+    return pltpu.with_memory_space_constraint(array, pltpu.HBM)
+
+
 def kept(array):
     return pltpu.with_memory_space_constraint(array, pltpu.VMEM)
 
@@ -211,11 +242,24 @@
     return pairs
 
 
-def exchange(a, b):
+def squares():
+    slabs, subs = lax.axis_size("slab"), lax.axis_size(SUB)
+    return [
+        [(i + p) * subs + j + q for p in (0, 1) for q in (0, 1)]
+        for i in range(0, slabs, 2)
+        for j in range(0, subs, 2)
+    ]
+
+
+def exchange(a, b, both):
     subs, slabs = lax.axis_size(SUB), lax.axis_size("slab")
     ao = lax.ppermute(a, SUB, swap(subs, 1))
+    bo = lax.ppermute(b, "slab", swap(slabs, 1))
+    if MODE == "square":
+        return ao, bo, lax.all_gather(both, SLAB_SUB, axis_index_groups=squares())
     be = lax.ppermute(b, "slab", swap(slabs, 0))
-    bo = lax.ppermute(b, "slab", swap(slabs, 1))
+    if MODE == "core":
+        return ao, be, bo, lax.all_gather(a, "sub_2")
     ae = lax.ppermute(a, SUB, swap(subs, 0))
     return ae, ao, be, bo
 
@@ -228,66 +272,63 @@
     lane = jnp.arange(LANES, dtype=jnp.int32)[None, :]
     position = jnp.stack([lax.axis_index(SUB), lax.axis_index("slab")])[:, None] % 2
     side = ((lane < 64) == (position == 0)).astype(jnp.int32)
+    side = jnp.concatenate([side, jnp.broadcast_to(position, side.shape)]).astype(jnp.int32)
 
     kept_f32 = lambda *shape: (shape, F32, "kept")
     kept_i32 = lambda *shape: (shape, jnp.int32, "kept")
-    table, w, send, a, b = call(
+    table, w, send, a, b, both = call(
         start_kernel,
-        "start",
         [kept_f32(24, nodes), kept_f32(8, nodes), kept_i32(2, LANES)]
-        + [kept_f32(24, LANES)] * 2,
-        near_null,
-        aggregates[None, :],
-        start_vector,
-        sends,
-    )
-    received = [kept(x) for x in exchange(a, b)]
+        + [kept_f32(24, LANES)] * 2
+        + [kept_f32(48, LANES)],
+        far(near_null),
+        far(aggregates[None, :]),
+        far(start_vector),
+        far(sends),
+    )
+    received = [kept(x) for x in exchange(a, b, both)]
     side = kept(side)
     scaled, index = call(
         blocks_kernel,
-        "blocks",
         [kept_f32(9, padded, nodes), kept_i32(padded, nodes)],
-        diag_block,
-        jnp.transpose(off_blocks, (1, 0, 2)),
-        columns,
+        far(diag_block),
+        far(jnp.transpose(off_blocks, (1, 0, 2))),
+        far(columns),
     )
     first_received = received
     for iteration in range(ITERS):
         last = iteration == ITERS - 1
         outs = [kept_f32(8, nodes)]
-        outs += [kept_f32(subs, LANES)] if last else [kept_f32(8, LANES)] * 2
+        outs += [kept_f32(subs, 1, LANES)] if last else [kept_f32(8, LANES)] * 2 + [kept_f32(16, LANES)]
         result = call(
             functools.partial(step_kernel, iteration == 0, last, subs),
-            f"step_{iteration}",
             outs,
             kept(scaled),
             kept(index),
             kept(w),
-            *received,
             side,
             kept(send),
+            *received,
         )
         w = result[0]
         if last:
             sums = result[1]
         else:
-            received = [kept(x) for x in exchange(result[1], result[2])]
+            received = [kept(x) for x in exchange(*result[1:])]
     (raw,) = call(
         blocks_out_kernel,
-        "blocks_out",
         [kept_f32(18, slots, nodes)],
         kept(scaled),
         kept(index),
         kept(table),
+        side,
         *first_received,
-        side,
     )
     sums = lax.all_to_all(sums, SUB, 0, 0, tiled=True)
-    (sums,) = call(regroup_kernel, "regroup", [kept_f32(slabs, LANES)], kept(sums))
+    (sums,) = call(regroup_kernel, [kept_f32(slabs, 1, LANES)], kept(sums))
     sums = lax.all_to_all(sums, "slab", 0, 0, tiled=True)
     prolong_off, prolong_self, rho = call(
         finish_kernel,
-        "finish",
         [((18, slots, nodes), jnp.bfloat16), ((18, nodes), jnp.bfloat16), ((1, LANES), F32)],
         kept(sums),
         kept(raw),

time: 173 us -> 153 us (0.88)
  starting transfers between devices: 120 us -> 39.8 us
  blocking collectives: 22.5 us -> 93.8 us
  waiting for transfers between devices: 13.6 us -> 6.87 us
  local copies, waits for them, and re-layouts: 6.12 us -> 0.07 us
  Pallas kernels: 7.97 us -> 10.6 us
    ppermute x16 -> x0, starting transfers between devices: 70.6 us -> none  [the longest x8 48.6 us: exchange(): be = lax.ppermute(b, 'slab', swap(slabs, 0))]
    all_gather x0 -> x8, blocking collectives: none -> 69.5 us  [exchange(): return (ao, bo, lax.all_gather(both, SLAB_SUB, axis_index_groups=squares()))]
    ppermute x8, starting transfers between devices: 34.9 us -> 26.4 us  [exchange(): ao = lax.ppermute(a, SUB, swap(subs, 1))]
    ppermute x16 -> x0, waiting for transfers between devices: 6.67 us -> none  [the longest x8 6.65 us: exchange(): be = lax.ppermute(b, 'slab', swap(slabs, 0))]
    unnamed x15 -> x0, local copies, waits for them, and re-layouts: 5.51 us -> none
    pallas_call x13, Pallas kernels: 7.97 us -> 10.6 us  [call(): pl.pallas_call(kernel, out_shape=[jax.ShapeDtypeStruct(*out) if len(out)...]
    all_to_all x1, blocking collectives: 22.5 us -> 24.3 us  [body(): sums = lax.all_to_all(sums, SUB, 0, 0, tiled=True)]
  transfers between devices with their start and end apart: 33 -> 17, of which waited for: 8 -> 1; matrix products, arithmetic and copies ran while one was open for 0% -> 0% of each run, Pallas kernels for 1% -> 2%
where the time goes in v1:
time: 153 us; the launch traced here: 152 us
  blocking collectives  93.8 us (61%)
  starting transfers between devices  39.8 us (26%)
  Pallas kernels  10.6 us (7%)
  waiting for transfers between devices  6.87 us (4%)
    all_gather x8, blocking collectives, exchange(): return (ao, bo, lax.all_gather(both, SLAB_SUB, axis_index_groups=squares()))  69.5 us
    ppermute x8, starting transfers between devices, exchange(): ao = lax.ppermute(a, SUB, swap(subs, 1))  26.4 us
    all_to_all x1, blocking collectives, body(): sums = lax.all_to_all(sums, SUB, 0, 0, tiled=True)  24.3 us
    pallas_call x13, Pallas kernels, call(): pl.pallas_call(kernel, out_shape=[jax.ShapeDtypeStruct(*out) if len(out)...  10.6 us
    all_to_all x1, starting transfers between devices, body(): sums = lax.all_to_all(sums, 'slab', 0, 0, tiled=True)  8.14 us
    all_to_all x1, waiting for transfers between devices, body(): sums = lax.all_to_all(sums, 'slab', 0, 0, tiled=True)  6.83 us
    ppermute x8, starting transfers between devices, exchange(): bo = lax.ppermute(b, 'slab', swap(slabs, 1))  5.29 us
  transfers between devices with their start and end apart: 17, of which 1 were waited for; matrix products, arithmetic and copies ran while one was open for 0% of the time, Pallas kernels for 2%

profile of v1, /device:TPU:1, one launch (start us, length us, event | category | flops | bytes accessed | tf_op | source)
XLA Modules:
  0.0 152.2 jit_solution(4910291016884889703)
XLA Ops:
  0.6 1.0 shard_map.95
  1.7 4.5 %collective-permute-start = (f32[24,128]{1,0:T(8,128)S(1)}, f32[24,128]{1,0:T(8,128)S(1)}, u32[]{:S(2)}, u32[]{:S(2)}) collective-permute-start(f32[24,128]{1,0:T(8,128)S(1)} %get-tuple-element.47), channel_id=1, source_target_pairs={{1,2},{2,1},{3,4},{4,3},{5,6},{6,5},{7,8},{8,7},{9,10},{10,9},{11,... | collective-permute-start | bytes 36872 | tf_op jit(solution)/shard_map/ppermute | solution.py:256
  7.2 11.8 %all-gather = f32[192,128]{1,0:T(8,128)S(1)} all-gather(f32[48,128]{1,0:T(8,128)S(1)} %get-tuple-element.49), channel_id=2, replica_groups={{0,1,64,65},{2,3,66,67},{4,5,68,69},{6,7,70,71},{8,9,72,73},{10,11,74,7..., dimensions={0}, use_global_device_ids=true | all-gather | bytes 122880 | tf_op jit(solution)/shard_map/all_gather | solution.py:259
  19.0 1.2 shard_map.94
  20.7 1.9 %collective-permute-start.2 = (f32[8,128]{1,0:T(8,128)S(1)}, f32[8,128]{1,0:T(8,128)S(1)}, u32[]{:S(2)}, u32[]{:S(2)}) collective-permute-start(f32[8,128]{1,0:T(8,128)S(1)} %get-tuple-element.51), channel_id=1, source_target_pairs={{1,2},{2,1},{3,4},{4,3},{5,6},{6,5},{7,8},{8,7},{9,10},{10,9},{11,... | collective-permute-start | bytes 12296 | tf_op jit(solution)/shard_map/ppermute | solution.py:256
  23.3 9.2 %all-gather.1 = f32[64,128]{1,0:T(8,128)S(1)} all-gather(f32[16,128]{1,0:T(8,128)S(1)} %get-tuple-element.53), channel_id=3, replica_groups={{0,1,64,65},{2,3,66,67},{4,5,68,69},{6,7,70,71},{8,9,72,73},{10,11,74,7..., dimensions={0}, use_global_device_ids=true | all-gather | bytes 40960 | tf_op jit(solution)/shard_map/all_gather | solution.py:259
  33.0 2.9 %collective-permute-start.4 = (f32[8,128]{1,0:T(8,128)S(1)}, f32[8,128]{1,0:T(8,128)S(1)}, u32[]{:S(2)}, u32[]{:S(2)}) collective-permute-start(f32[8,128]{1,0:T(8,128)S(1)} %get-tuple-element.55), channel_id=1, source_target_pairs={{1,2},{2,1},{3,4},{4,3},{5,6},{6,5},{7,8},{8,7},{9,10},{10,9},{11,... | collective-permute-start | bytes 12296 | tf_op jit(solution)/shard_map/ppermute | solution.py:256
  36.6 9.2 %all-gather.2 = f32[64,128]{1,0:T(8,128)S(1)} all-gather(f32[16,128]{1,0:T(8,128)S(1)} %get-tuple-element.57), channel_id=4, replica_groups={{0,1,64,65},{2,3,66,67},{4,5,68,69},{6,7,70,71},{8,9,72,73},{10,11,74,7..., dimensions={0}, use_global_device_ids=true | all-gather | bytes 40960 | tf_op jit(solution)/shard_map/all_gather | solution.py:259
  46.3 3.2 %collective-permute-start.6 = (f32[8,128]{1,0:T(8,128)S(1)}, f32[8,128]{1,0:T(8,128)S(1)}, u32[]{:S(2)}, u32[]{:S(2)}) collective-permute-start(f32[8,128]{1,0:T(8,128)S(1)} %get-tuple-element.59), channel_id=1, source_target_pairs={{1,2},{2,1},{3,4},{4,3},{5,6},{6,5},{7,8},{8,7},{9,10},{10,9},{11,... | collective-permute-start | bytes 12296 | tf_op jit(solution)/shard_map/ppermute | solution.py:256
  50.1 8.0 %all-gather.3 = f32[64,128]{1,0:T(8,128)S(1)} all-gather(f32[16,128]{1,0:T(8,128)S(1)} %get-tuple-element.61), channel_id=5, replica_groups={{0,1,64,65},{2,3,66,67},{4,5,68,69},{6,7,70,71},{8,9,72,73},{10,11,74,7..., dimensions={0}, use_global_device_ids=true | all-gather | bytes 40960 | tf_op jit(solution)/shard_map/all_gather | solution.py:259
  58.6 4.0 %collective-permute-start.8 = (f32[8,128]{1,0:T(8,128)S(1)}, f32[8,128]{1,0:T(8,128)S(1)}, u32[]{:S(2)}, u32[]{:S(2)}) collective-permute-start(f32[8,128]{1,0:T(8,128)S(1)} %get-tuple-element.63), channel_id=1, source_target_pairs={{1,2},{2,1},{3,4},{4,3},{5,6},{6,5},{7,8},{8,7},{9,10},{10,9},{11,... | collective-permute-start | bytes 12296 | tf_op jit(solution)/shard_map/ppermute | solution.py:256
  63.3 8.2 %all-gather.4 = f32[64,128]{1,0:T(8,128)S(1)} all-gather(f32[16,128]{1,0:T(8,128)S(1)} %get-tuple-element.65), channel_id=6, replica_groups={{0,1,64,65},{2,3,66,67},{4,5,68,69},{6,7,70,71},{8,9,72,73},{10,11,74,7..., dimensions={0}, use_global_device_ids=true | all-gather | bytes 40960 | tf_op jit(solution)/shard_map/all_gather | solution.py:259
  72.0 3.1 %collective-permute-start.10 = (f32[8,128]{1,0:T(8,128)S(1)}, f32[8,128]{1,0:T(8,128)S(1)}, u32[]{:S(2)}, u32[]{:S(2)}) collective-permute-start(f32[8,128]{1,0:T(8,128)S(1)} %get-tuple-element.67), channel_id=1, source_target_pairs={{1,2},{2,1},{3,4},{4,3},{5,6},{6,5},{7,8},{8,7},{9,10},{10,9},{11,... | collective-permute-start | bytes 12296 | tf_op jit(solution)/shard_map/ppermute | solution.py:256
  75.8 7.7 %all-gather.5 = f32[64,128]{1,0:T(8,128)S(1)} all-gather(f32[16,128]{1,0:T(8,128)S(1)} %get-tuple-element.69), channel_id=7, replica_groups={{0,1,64,65},{2,3,66,67},{4,5,68,69},{6,7,70,71},{8,9,72,73},{10,11,74,7..., dimensions={0}, use_global_device_ids=true | all-gather | bytes 40960 | tf_op jit(solution)/shard_map/all_gather | solution.py:259
  84.0 3.6 %collective-permute-start.12 = (f32[8,128]{1,0:T(8,128)S(1)}, f32[8,128]{1,0:T(8,128)S(1)}, u32[]{:S(2)}, u32[]{:S(2)}) collective-permute-start(f32[8,128]{1,0:T(8,128)S(1)} %get-tuple-element.71), channel_id=1, source_target_pairs={{1,2},{2,1},{3,4},{4,3},{5,6},{6,5},{7,8},{8,7},{9,10},{10,9},{11,... | collective-permute-start | bytes 12296 | tf_op jit(solution)/shard_map/ppermute | solution.py:256
  88.3 7.9 %all-gather.6 = f32[64,128]{1,0:T(8,128)S(1)} all-gather(f32[16,128]{1,0:T(8,128)S(1)} %get-tuple-element.73), channel_id=8, replica_groups={{0,1,64,65},{2,3,66,67},{4,5,68,69},{6,7,70,71},{8,9,72,73},{10,11,74,7..., dimensions={0}, use_global_device_ids=true | all-gather | bytes 40960 | tf_op jit(solution)/shard_map/all_gather | solution.py:259
  96.7 3.2 %collective-permute-start.14 = (f32[8,128]{1,0:T(8,128)S(1)}, f32[8,128]{1,0:T(8,128)S(1)}, u32[]{:S(2)}, u32[]{:S(2)}) collective-permute-start(f32[8,128]{1,0:T(8,128)S(1)} %get-tuple-element.75), channel_id=1, source_target_pairs={{1,2},{2,1},{3,4},{4,3},{5,6},{6,5},{7,8},{8,7},{9,10},{10,9},{11,... | collective-permute-start | bytes 12296 | tf_op jit(solution)/shard_map/ppermute | solution.py:256
  100.7 7.5 %all-gather.7 = f32[64,128]{1,0:T(8,128)S(1)} all-gather(f32[16,128]{1,0:T(8,128)S(1)} %get-tuple-element.77), channel_id=9, replica_groups={{0,1,64,65},{2,3,66,67},{4,5,68,69},{6,7,70,71},{8,9,72,73},{10,11,74,7..., dimensions={0}, use_global_device_ids=true | all-gather | bytes 40960 | tf_op jit(solution)/shard_map/all_gather | solution.py:259
  108.2 1.1 shard_map.103
  109.2 24.3 %all_to_all.10.sums_ref = f32[64,1,128]{2,1,0:T(1,128)S(1)} all-to-all(f32[64,1,128]{2,1,0:T(1,128)S(1)} %get-tuple-element.78), channel_id=1, replica_groups=mesh['slab'=12,'sub_0'=8,'sub_1'=4,'sub_2'=2] {'sub_0','sub_1','sub_2'}, dimensions={0} | all-to-all | bytes 65536 | tf_op jit(solution)/shard_map/all_to_all | solution.py:327
  134.2 8.1 %all-to-all-start.1 = ((f32[12,1,128]{2,1,0:T(1,128)}), f32[12,1,128]{2,1,0:T(1,128)S(1)}, u32[]{:S(2)}, u32[]{:S(2)}) async-start(f32[12,1,128]{2,1,0:T(1,128)} %shard_map.104), calls=%async_computation.1 | async-start | bytes 12288 | tf_op jit(solution)/shard_map/all_to_all | solution.py:329
  142.3 2.0 %shard_map.105.raw_ref = f32[18,26,512]{2,1,0:T(8,128)S(1)} custom-call(f32[9,32,512]{2,1,0:T(8,128)S(1)} %get-tuple-element.43.refs_0_.scaled_ref, s32[32,512]{1,0:T(8,128)S(1)} %get-tuple-element.44.refs_1_.index_ref, f32[24,512]{1,0:T(8,128)S(1)} %get-tuple-element.79.table_ref, s32[4,128]{1,0:T(4,128)S(1)} %pad_add_fusion.refs_3_.side_ref, ...), custom_call_target="tpu_custom_call" | custom-call | tf_op jit(solution)/shard_map/pallas_call | solution.py:219
  144.4 6.8 %all-to-all-done.1.sums_ref = f32[12,1,128]{2,1,0:T(1,128)S(1)} async-done(((f32[12,1,128]{2,1,0:T(1,128)}), f32[12,1,128]{2,1,0:T(1,128)S(1)}, u32[]{:S(2)}, u32[]{:S(2)}) %all-to-all-start.1) | async-done | bytes 6176 | tf_op jit(solution)/shard_map/all_to_all | solution.py:329
  151.2 1.0 shard_map.106
  (37 shorter events, 9.9 us)
Async XLA Ops:
  1.7 18.5 %collective-permute-start = (f32[24,128]{1,0:T(8,128)S(1)}, f32[24,128]{1,0:T(8,128)S(1)}, u32[]{:S(2)}, u32[]{:S(2)}) collective-permute-start(f32[24,128]{1,0:T(8,128)S(1)} %get-tuple-element.47), channel_id=1, source_target_pairs={{1,2},{2,1},{3,4},{4,3},{5,6},{6,5},{7,8},{8,7},{9,10},{10,9},{11,... | collective-permute-start | bytes 36872 | tf_op jit(solution)/shard_map/ppermute | solution.py:256
  6.2 14.0 %collective-permute-start.1 = (f32[24,128]{1,0:T(8,128)S(1)}, f32[24,128]{1,0:T(8,128)S(1)}, u32[]{:S(2)}, u32[]{:S(2)}) collective-permute-start(f32[24,128]{1,0:T(8,128)S(1)} %get-tuple-element.48), channel_id=1, source_target_pairs={{64,128},{128,64},{192,256},{256,192},{320,384},{384,320},{448,512... | collective-permute-start | bytes 36872 | tf_op jit(solution)/shard_map/ppermute | solution.py:257
  20.7 11.8 %collective-permute-start.2 = (f32[8,128]{1,0:T(8,128)S(1)}, f32[8,128]{1,0:T(8,128)S(1)}, u32[]{:S(2)}, u32[]{:S(2)}) collective-permute-start(f32[8,128]{1,0:T(8,128)S(1)} %get-tuple-element.51), channel_id=1, source_target_pairs={{1,2},{2,1},{3,4},{4,3},{5,6},{6,5},{7,8},{8,7},{9,10},{10,9},{11,... | collective-permute-start | bytes 12296 | tf_op jit(solution)/shard_map/ppermute | solution.py:256
  22.6 9.9 %collective-permute-start.3 = (f32[8,128]{1,0:T(8,128)S(1)}, f32[8,128]{1,0:T(8,128)S(1)}, u32[]{:S(2)}, u32[]{:S(2)}) collective-permute-start(f32[8,128]{1,0:T(8,128)S(1)} %get-tuple-element.52), channel_id=1, source_target_pairs={{64,128},{128,64},{192,256},{256,192},{320,384},{384,320},{448,512... | collective-permute-start | bytes 12296 | tf_op jit(solution)/shard_map/ppermute | solution.py:257
  33.0 12.8 %collective-permute-start.4 = (f32[8,128]{1,0:T(8,128)S(1)}, f32[8,128]{1,0:T(8,128)S(1)}, u32[]{:S(2)}, u32[]{:S(2)}) collective-permute-start(f32[8,128]{1,0:T(8,128)S(1)} %get-tuple-element.55), channel_id=1, source_target_pairs={{1,2},{2,1},{3,4},{4,3},{5,6},{6,5},{7,8},{8,7},{9,10},{10,9},{11,... | collective-permute-start | bytes 12296 | tf_op jit(solution)/shard_map/ppermute | solution.py:256
  35.9 9.9 %collective-permute-start.5 = (f32[8,128]{1,0:T(8,128)S(1)}, f32[8,128]{1,0:T(8,128)S(1)}, u32[]{:S(2)}, u32[]{:S(2)}) collective-permute-start(f32[8,128]{1,0:T(8,128)S(1)} %get-tuple-element.56), channel_id=1, source_target_pairs={{64,128},{128,64},{192,256},{256,192},{320,384},{384,320},{448,512... | collective-permute-start | bytes 12296 | tf_op jit(solution)/shard_map/ppermute | solution.py:257
  46.3 11.9 %collective-permute-start.6 = (f32[8,128]{1,0:T(8,128)S(1)}, f32[8,128]{1,0:T(8,128)S(1)}, u32[]{:S(2)}, u32[]{:S(2)}) collective-permute-start(f32[8,128]{1,0:T(8,128)S(1)} %get-tuple-element.59), channel_id=1, source_target_pairs={{1,2},{2,1},{3,4},{4,3},{5,6},{6,5},{7,8},{8,7},{9,10},{10,9},{11,... | collective-permute-start | bytes 12296 | tf_op jit(solution)/shard_map/ppermute | solution.py:256
  49.4 8.7 %collective-permute-start.7 = (f32[8,128]{1,0:T(8,128)S(1)}, f32[8,128]{1,0:T(8,128)S(1)}, u32[]{:S(2)}, u32[]{:S(2)}) collective-permute-start(f32[8,128]{1,0:T(8,128)S(1)} %get-tuple-element.60), channel_id=1, source_target_pairs={{64,128},{128,64},{192,256},{256,192},{320,384},{384,320},{448,512... | collective-permute-start | bytes 12296 | tf_op jit(solution)/shard_map/ppermute | solution.py:257
  58.6 12.9 %collective-permute-start.8 = (f32[8,128]{1,0:T(8,128)S(1)}, f32[8,128]{1,0:T(8,128)S(1)}, u32[]{:S(2)}, u32[]{:S(2)}) collective-permute-start(f32[8,128]{1,0:T(8,128)S(1)} %get-tuple-element.63), channel_id=1, source_target_pairs={{1,2},{2,1},{3,4},{4,3},{5,6},{6,5},{7,8},{8,7},{9,10},{10,9},{11,... | collective-permute-start | bytes 12296 | tf_op jit(solution)/shard_map/ppermute | solution.py:256
  62.7 8.9 %collective-permute-start.9 = (f32[8,128]{1,0:T(8,128)S(1)}, f32[8,128]{1,0:T(8,128)S(1)}, u32[]{:S(2)}, u32[]{:S(2)}) collective-permute-start(f32[8,128]{1,0:T(8,128)S(1)} %get-tuple-element.64), channel_id=1, source_target_pairs={{64,128},{128,64},{192,256},{256,192},{320,384},{384,320},{448,512... | collective-permute-start | bytes 12296 | tf_op jit(solution)/shard_map/ppermute | solution.py:257
  72.0 11.4 %collective-permute-start.10 = (f32[8,128]{1,0:T(8,128)S(1)}, f32[8,128]{1,0:T(8,128)S(1)}, u32[]{:S(2)}, u32[]{:S(2)}) collective-permute-start(f32[8,128]{1,0:T(8,128)S(1)} %get-tuple-element.67), channel_id=1, source_target_pairs={{1,2},{2,1},{3,4},{4,3},{5,6},{6,5},{7,8},{8,7},{9,10},{10,9},{11,... | collective-permute-start | bytes 12296 | tf_op jit(solution)/shard_map/ppermute | solution.py:256
  75.1 8.4 %collective-permute-start.11 = (f32[8,128]{1,0:T(8,128)S(1)}, f32[8,128]{1,0:T(8,128)S(1)}, u32[]{:S(2)}, u32[]{:S(2)}) collective-permute-start(f32[8,128]{1,0:T(8,128)S(1)} %get-tuple-element.68), channel_id=1, source_target_pairs={{64,128},{128,64},{192,256},{256,192},{320,384},{384,320},{448,512... | collective-permute-start | bytes 12296 | tf_op jit(solution)/shard_map/ppermute | solution.py:257
  84.0 12.3 %collective-permute-start.12 = (f32[8,128]{1,0:T(8,128)S(1)}, f32[8,128]{1,0:T(8,128)S(1)}, u32[]{:S(2)}, u32[]{:S(2)}) collective-permute-start(f32[8,128]{1,0:T(8,128)S(1)} %get-tuple-element.71), channel_id=1, source_target_pairs={{1,2},{2,1},{3,4},{4,3},{5,6},{6,5},{7,8},{8,7},{9,10},{10,9},{11,... | collective-permute-start | bytes 12296 | tf_op jit(solution)/shard_map/ppermute | solution.py:256
  87.6 8.6 %collective-permute-start.13 = (f32[8,128]{1,0:T(8,128)S(1)}, f32[8,128]{1,0:T(8,128)S(1)}, u32[]{:S(2)}, u32[]{:S(2)}) collective-permute-start(f32[8,128]{1,0:T(8,128)S(1)} %get-tuple-element.72), channel_id=1, source_target_pairs={{64,128},{128,64},{192,256},{256,192},{320,384},{384,320},{448,512... | collective-permute-start | bytes 12296 | tf_op jit(solution)/shard_map/ppermute | solution.py:257
  96.7 11.4 %collective-permute-start.14 = (f32[8,128]{1,0:T(8,128)S(1)}, f32[8,128]{1,0:T(8,128)S(1)}, u32[]{:S(2)}, u32[]{:S(2)}) collective-permute-start(f32[8,128]{1,0:T(8,128)S(1)} %get-tuple-element.75), channel_id=1, source_target_pairs={{1,2},{2,1},{3,4},{4,3},{5,6},{6,5},{7,8},{8,7},{9,10},{10,9},{11,... | collective-permute-start | bytes 12296 | tf_op jit(solution)/shard_map/ppermute | solution.py:256
  100.0 8.2 %collective-permute-start.15 = (f32[8,128]{1,0:T(8,128)S(1)}, f32[8,128]{1,0:T(8,128)S(1)}, u32[]{:S(2)}, u32[]{:S(2)}) collective-permute-start(f32[8,128]{1,0:T(8,128)S(1)} %get-tuple-element.76), channel_id=1, source_target_pairs={{64,128},{128,64},{192,256},{256,192},{320,384},{384,320},{448,512... | collective-permute-start | bytes 12296 | tf_op jit(solution)/shard_map/ppermute | solution.py:257
  134.2 17.0 %all-to-all-start.1 = ((f32[12,1,128]{2,1,0:T(1,128)}), f32[12,1,128]{2,1,0:T(1,128)S(1)}, u32[]{:S(2)}, u32[]{:S(2)}) async-start(f32[12,1,128]{2,1,0:T(1,128)} %shard_map.104), calls=%async_computation.1 | async-start | bytes 12288 | tf_op jit(solution)/shard_map/all_to_all | solution.py:329

commit v2 on v1

--- a/solution.py
+++ b/solution.py
@@ -14,9 +14,9 @@
 SLAB_SUB = ("slab", "sub_0", "sub_1", "sub_2")
 LANES = 128
 F32 = jnp.float32
-MODE = "square"
-RECEIVED = {"perm": 4, "core": 4, "square": 3}[MODE]
+RECEIVED = 3
 VM = pl.BlockSpec(memory_space=pltpu.VMEM)
+HB = pl.BlockSpec(memory_space=pltpu.HBM)
 
 
 def lanes(group):
@@ -47,7 +47,19 @@
     both_ref[tiles * 8 :, :] = pay_refs[1][...]
 
 
-def start_kernel(near_ref, aggregates_ref, start_ref, sends_ref, table_ref, w_ref, send_ref, a_ref, b_ref, both_ref):
+def start_kernel(*refs):
+    far_refs, refs = refs[:7], refs[7:]
+    table_ref, w_ref, send_ref, a_ref, b_ref, both_ref, scaled_ref, index_ref = refs[:8]
+    near_refs, sems = refs[8:15], refs[15:]
+    copies = [
+        pltpu.make_async_copy(source, target, sem)
+        for source, target, sem in zip(far_refs, near_refs, sems)
+    ]
+    for copy in copies:
+        copy.start()
+    near_ref, aggregates_ref, start_ref, sends_ref, diag_ref, off_ref, columns_ref = near_refs
+    for copy in copies[:4]:
+        copy.wait()
     nodes = near_ref.shape[1]
     groups = nodes // 8
     for e in range(4):
@@ -63,9 +75,8 @@
         table_ref[row * 8 + 6 : row * 8 + 7, :] = start_ref[row : row + 1, :]
     w_ref[0:3, :] = start_ref[...]
     pack_rows(table_ref, 3, send_ref, (a_ref, b_ref), both_ref)
-
-
-def blocks_kernel(diag_ref, off_ref, columns_ref, scaled_ref, index_ref):
+    for copy in copies[4:]:
+        copy.wait()
     slots = off_ref.shape[1]
     index_ref[0:slots, :] = columns_ref[...]
     index_ref[slots:, :] = jnp.zeros((index_ref.shape[0] - slots, index_ref.shape[1]), jnp.int32)
@@ -98,44 +109,31 @@
 
 
 def ghost_rows(refs, side_ref, row):
-    if MODE == "perm":
-        ae, ao, be, bo = refs
-        even = ae[row, :], be[row, :]
-        odd = ao[row, :], bo[row, :]
-    elif MODE == "core":
-        ao, be, bo, gathered = refs
-        odd_sub = side_ref[2:3, :] != 0
-        even = jnp.where(odd_sub, gathered[0, row, :], gathered[1, row, :]), be[row, :]
-        odd = ao[row, :], bo[row, :]
-    else:
-        ao, bo, gathered = refs
-        odd_sub = side_ref[2:3, :] != 0
-        odd_slab = side_ref[3:4, :] != 0
-        half = gathered.shape[1] // 2
-        down = slice(row.start + half, row.stop + half)
-        even_a = jnp.where(
-            odd_slab,
-            jnp.where(odd_sub, gathered[2, row, :], gathered[3, row, :]),
-            jnp.where(odd_sub, gathered[0, row, :], gathered[1, row, :]),
-        )
-        even_b = jnp.where(
-            odd_slab,
-            jnp.where(odd_sub, gathered[1, down, :], gathered[0, down, :]),
-            jnp.where(odd_sub, gathered[3, down, :], gathered[2, down, :]),
-        )
-        even = even_a, even_b
-        odd = ao[row, :], bo[row, :]
+    ao, bo, gathered = refs
+    odd_sub = side_ref[2:3, :] != 0
+    odd_slab = side_ref[3:4, :] != 0
+    half = gathered.shape[1] // 2
+    down = slice(row.start + half, row.stop + half)
+    even_a = jnp.where(
+        odd_slab,
+        jnp.where(odd_sub, gathered[2, row, :], gathered[3, row, :]),
+        jnp.where(odd_sub, gathered[0, row, :], gathered[1, row, :]),
+    )
+    even_b = jnp.where(
+        odd_slab,
+        jnp.where(odd_sub, gathered[1, down, :], gathered[0, down, :]),
+        jnp.where(odd_sub, gathered[3, down, :], gathered[2, down, :]),
+    )
     return [
-        spread(jnp.where(side_ref[axis : axis + 1, :] != 0, odd[axis], even[axis]))
-        for axis in range(2)
-    ]
-
-
-def step_kernel(first, last, count, *refs):
+        spread(jnp.where(side_ref[0:1, :] != 0, ao[row, :], even_a)),
+        spread(jnp.where(side_ref[1:2, :] != 0, bo[row, :], even_b)),
+    ]
+
+
+def step_kernel(first, last, *refs):
     scaled_ref, index_ref, w_ref, side_ref, send_ref = refs[:5]
     received = refs[5 : 5 + RECEIVED]
     outs = refs[5 + RECEIVED :]
-    next_ref = outs[0]
     table = []
     for c in range(3):
         row = c * 8 + 6 if first else c
@@ -143,7 +141,9 @@
             [spread(w_ref[c : c + 1, lanes(group)]) for group in range(4)]
             + ghost_rows(received, side_ref, slice(row, row + 1))
         )
-    next_ref[...] = jnp.zeros(next_ref.shape, F32)
+    if not last:
+        outs[0][...] = jnp.zeros(outs[0].shape, F32)
+    latest = jnp.zeros((1, LANES), F32)
     for block in range(4):
         total = [None] * 3
         for tile in range(4):
@@ -156,18 +156,26 @@
                     term = scaled_ref[r * 3 + c, slots, lanes(block)] * found
                     total[r] = term if total[r] is None else total[r] + term
         for r in range(3):
-            next_ref[r : r + 1, lanes(block)] = w_ref[r : r + 1, lanes(block)] + jnp.sum(
-                total[r], axis=0, keepdims=True
-            )
+            new = w_ref[r : r + 1, lanes(block)] + jnp.sum(total[r], axis=0, keepdims=True)
+            if last:
+                latest = latest + new * new
+            else:
+                outs[0][r : r + 1, lanes(block)] = new
     if last:
-        sums_ref = outs[1]
-        latest = jnp.sum(next_ref[...] * next_ref[...], keepdims=True)
-        earlier = jnp.sum(w_ref[...] * w_ref[...], keepdims=True)
+        (sums_ref,) = outs
+        earlier = jnp.zeros((8, LANES), F32)
+        for block in range(4):
+            old = w_ref[:, lanes(block)]
+            earlier = earlier + old * old
+        earlier = jnp.sum(earlier, axis=0, keepdims=True)
+        count = sums_ref.shape[0]
+        latest = latest + pltpu.roll(latest, 64, 1)
+        earlier = earlier + pltpu.roll(earlier, 64, 1)
         lane = lax.broadcasted_iota(jnp.int32, (1, LANES), 1)
-        both = jnp.where(lane == 0, latest, jnp.where(lane == 1, earlier, 0.0))
+        both = jnp.where(lane < 64, latest, earlier)
         sums_ref[...] = jnp.broadcast_to(both[None], (count, 1, LANES))
     else:
-        pack_rows(next_ref, 1, send_ref, outs[1:3], outs[3])
+        pack_rows(outs[0], 1, send_ref, outs[1:3], outs[3])
 
 
 def blocks_out_kernel(scaled_ref, index_ref, table_ref, side_ref, *refs):
@@ -201,8 +209,8 @@
 def finish_kernel(sums_ref, raw_ref, table_ref, off_ref, self_ref, rho_ref):
     total = jnp.sum(sums_ref[...], axis=0)
     lane = lax.broadcasted_iota(jnp.int32, (1, LANES), 1)
-    latest = jnp.sum(jnp.where(lane == 0, total, 0.0), keepdims=True)
-    earlier = jnp.sum(jnp.where(lane == 1, total, 0.0), keepdims=True)
+    latest = jnp.sum(jnp.where(lane < 64, total, 0.0), axis=1, keepdims=True)
+    earlier = jnp.sum(jnp.where(lane < 64, 0.0, total), axis=1, keepdims=True)
     rho = jnp.sqrt(latest / (earlier + 1e-05))
     rho_ref[...] = jnp.broadcast_to(rho, rho_ref.shape)
     factor = -(OMEGA / rho)
@@ -215,14 +223,17 @@
         )
 
 
-def call(kernel, outs, *args):
+def call(kernel, name, outs, *args, near=None, scratch=()):
+    near = len(args) if near is None else near
     return pl.pallas_call(
         kernel,
+        name=name,
         out_shape=[
             jax.ShapeDtypeStruct(*out) if len(out) == 2 else pltpu.VMEM(*out[:2]) for out in outs
         ],
-        in_specs=[VM] * len(args),
+        in_specs=[VM] * near + [HB] * (len(args) - near),
         out_specs=[VM] * len(outs),
+        scratch_shapes=list(scratch),
         compiler_params=pltpu.CompilerParams(vmem_limit_bytes=16 << 20),
     )(*args)
 
@@ -252,16 +263,9 @@
 
 
 def exchange(a, b, both):
-    subs, slabs = lax.axis_size(SUB), lax.axis_size("slab")
-    ao = lax.ppermute(a, SUB, swap(subs, 1))
-    bo = lax.ppermute(b, "slab", swap(slabs, 1))
-    if MODE == "square":
-        return ao, bo, lax.all_gather(both, SLAB_SUB, axis_index_groups=squares())
-    be = lax.ppermute(b, "slab", swap(slabs, 0))
-    if MODE == "core":
-        return ao, be, bo, lax.all_gather(a, "sub_2")
-    ae = lax.ppermute(a, SUB, swap(subs, 0))
-    return ae, ao, be, bo
+    bo = lax.ppermute(b, "slab", swap(lax.axis_size("slab"), 1))
+    ao = lax.ppermute(a, SUB, swap(lax.axis_size(SUB), 1))
+    return ao, bo, lax.all_gather(both, SLAB_SUB, axis_index_groups=squares())
 
 
 def body(near_null, aggregates, diag_block, off_blocks, columns, sends, start_vector):
@@ -276,32 +280,42 @@
 
     kept_f32 = lambda *shape: (shape, F32, "kept")
     kept_i32 = lambda *shape: (shape, jnp.int32, "kept")
-    table, w, send, a, b, both = call(
+    table, w, send, a, b, both, scaled, index = call(
         start_kernel,
+        "start",
         [kept_f32(24, nodes), kept_f32(8, nodes), kept_i32(2, LANES)]
         + [kept_f32(24, LANES)] * 2
-        + [kept_f32(48, LANES)],
+        + [kept_f32(48, LANES), kept_f32(9, padded, nodes), kept_i32(padded, nodes)],
         far(near_null),
         far(aggregates[None, :]),
         far(start_vector),
         far(sends),
-    )
-    received = [kept(x) for x in exchange(a, b, both)]
-    side = kept(side)
-    scaled, index = call(
-        blocks_kernel,
-        [kept_f32(9, padded, nodes), kept_i32(padded, nodes)],
         far(diag_block),
         far(jnp.transpose(off_blocks, (1, 0, 2))),
         far(columns),
-    )
+        near=0,
+        scratch=[
+            pltpu.VMEM((18, nodes), F32),
+            pltpu.VMEM((1, nodes), jnp.int32),
+            pltpu.VMEM((3, nodes), F32),
+            pltpu.VMEM((4, 64), jnp.int32),
+            pltpu.VMEM((9, nodes), F32),
+            pltpu.VMEM((9, slots, nodes), F32),
+            pltpu.VMEM((slots, nodes), jnp.int32),
+        ]
+        + [pltpu.SemaphoreType.DMA] * 7,
+    )
+    received = [kept(x) for x in exchange(a, b, both)]
+    side = kept(side)
     first_received = received
     for iteration in range(ITERS):
         last = iteration == ITERS - 1
-        outs = [kept_f32(8, nodes)]
-        outs += [kept_f32(subs, 1, LANES)] if last else [kept_f32(8, LANES)] * 2 + [kept_f32(16, LANES)]
+        outs = [kept_f32(8, nodes)] + [kept_f32(8, LANES)] * 2 + [kept_f32(16, LANES)]
+        if last:
+            outs = [kept_f32(subs, 1, LANES)]
         result = call(
-            functools.partial(step_kernel, iteration == 0, last, subs),
+            functools.partial(step_kernel, iteration == 0, last),
+            f"step_{iteration}",
             outs,
             kept(scaled),
             kept(index),
@@ -310,13 +324,14 @@
             kept(send),
             *received,
         )
-        w = result[0]
         if last:
-            sums = result[1]
+            (sums,) = result
         else:
+            w = result[0]
             received = [kept(x) for x in exchange(*result[1:])]
     (raw,) = call(
         blocks_out_kernel,
+        "blocks_out",
         [kept_f32(18, slots, nodes)],
         kept(scaled),
         kept(index),
@@ -325,10 +340,11 @@
         *first_received,
     )
     sums = lax.all_to_all(sums, SUB, 0, 0, tiled=True)
-    (sums,) = call(regroup_kernel, [kept_f32(slabs, 1, LANES)], kept(sums))
+    (sums,) = call(regroup_kernel, "regroup", [kept_f32(slabs, 1, LANES)], kept(sums))
     sums = lax.all_to_all(sums, "slab", 0, 0, tiled=True)
     prolong_off, prolong_self, rho = call(
         finish_kernel,
+        "finish",
         [((18, slots, nodes), jnp.bfloat16), ((18, nodes), jnp.bfloat16), ((1, LANES), F32)],
         kept(sums),
         kept(raw),

time: 153 us -> 151 us (0.987)
    pallas_call x13 -> x12, Pallas kernels: 10.6 us -> 9.16 us  [call(): pl.pallas_call(kernel, name=name, out_shape=[jax.ShapeDtypeStruct(*out) i...]
  transfers between devices with their start and end apart: 17 -> 17, of which waited for: 1 -> 1; matrix products, arithmetic and copies ran while one was open for 0% -> 0% of each run, Pallas kernels for 2% -> 1%
where the time goes in v2:
time: 151 us
  blocking collectives  93.8 us (62%)
  starting transfers between devices  39.8 us (26%)
  Pallas kernels  9.16 us (6%)
  waiting for transfers between devices  6.87 us (5%)
    all_gather x8, blocking collectives, exchange(): return (ao, bo, lax.all_gather(both, SLAB_SUB, axis_index_groups=squares()))  69.5 us
    ppermute x8, starting transfers between devices, exchange(): ao = lax.ppermute(a, SUB, swap(lax.axis_size(SUB), 1))  26.4 us
    all_to_all x1, blocking collectives, body(): sums = lax.all_to_all(sums, SUB, 0, 0, tiled=True)  24.3 us
    pallas_call x12, Pallas kernels, call(): pl.pallas_call(kernel, name=name, out_shape=[jax.ShapeDtypeStruct(*out) i...  9.16 us
    all_to_all x1, starting transfers between devices, body(): sums = lax.all_to_all(sums, 'slab', 0, 0, tiled=True)  8.14 us
    all_to_all x1, waiting for transfers between devices, body(): sums = lax.all_to_all(sums, 'slab', 0, 0, tiled=True)  6.83 us
    ppermute x8, starting transfers between devices, exchange(): bo = lax.ppermute(b, 'slab', swap(lax.axis_size('slab'), 1))  5.29 us
  transfers between devices with their start and end apart: 17, of which 1 were waited for; matrix products, arithmetic and copies ran while one was open for 0% of the time, Pallas kernels for 1%

profile of v2, /device:TPU:1, one launch (start us, length us, event | category | flops | bytes accessed | tf_op | source)
XLA Modules:
  0.0 150.8 jit_solution(3027140127170059852)
XLA Ops:
  0.6 1.4 start.1
  2.0 4.5 %collective-permute-start = (f32[24,128]{1,0:T(8,128)S(1)}, f32[24,128]{1,0:T(8,128)S(1)}, u32[]{:S(2)}, u32[]{:S(2)}) collective-permute-start(f32[24,128]{1,0:T(8,128)S(1)} %get-tuple-element.46), channel_id=1, source_target_pairs={{1,2},{2,1},{3,4},{4,3},{5,6},{6,5},{7,8},{8,7},{9,10},{10,9},{11,... | collective-permute-start | bytes 36872 | tf_op jit(solution)/shard_map/ppermute | solution.py:267
  6.5 0.7 collective-permute-start.1
  7.5 11.8 %all-gather = f32[192,128]{1,0:T(8,128)S(1)} all-gather(f32[48,128]{1,0:T(8,128)S(1)} %get-tuple-element.48), channel_id=2, replica_groups={{0,1,64,65},{2,3,66,67},{4,5,68,69},{6,7,70,71},{8,9,72,73},{10,11,74,7..., dimensions={0}, use_global_device_ids=true | all-gather | bytes 122880 | tf_op jit(solution)/shard_map/all_gather | solution.py:268
  19.8 1.9 %collective-permute-start.2 = (f32[8,128]{1,0:T(8,128)S(1)}, f32[8,128]{1,0:T(8,128)S(1)}, u32[]{:S(2)}, u32[]{:S(2)}) collective-permute-start(f32[8,128]{1,0:T(8,128)S(1)} %get-tuple-element.50), channel_id=1, source_target_pairs={{1,2},{2,1},{3,4},{4,3},{5,6},{6,5},{7,8},{8,7},{9,10},{10,9},{11,... | collective-permute-start | bytes 12296 | tf_op jit(solution)/shard_map/ppermute | solution.py:267
  22.4 9.2 %all-gather.1 = f32[64,128]{1,0:T(8,128)S(1)} all-gather(f32[16,128]{1,0:T(8,128)S(1)} %get-tuple-element.52), channel_id=3, replica_groups={{0,1,64,65},{2,3,66,67},{4,5,68,69},{6,7,70,71},{8,9,72,73},{10,11,74,7..., dimensions={0}, use_global_device_ids=true | all-gather | bytes 40960 | tf_op jit(solution)/shard_map/all_gather | solution.py:268
  32.1 2.9 %collective-permute-start.4 = (f32[8,128]{1,0:T(8,128)S(1)}, f32[8,128]{1,0:T(8,128)S(1)}, u32[]{:S(2)}, u32[]{:S(2)}) collective-permute-start(f32[8,128]{1,0:T(8,128)S(1)} %get-tuple-element.54), channel_id=1, source_target_pairs={{1,2},{2,1},{3,4},{4,3},{5,6},{6,5},{7,8},{8,7},{9,10},{10,9},{11,... | collective-permute-start | bytes 12296 | tf_op jit(solution)/shard_map/ppermute | solution.py:267
  35.7 9.2 %all-gather.2 = f32[64,128]{1,0:T(8,128)S(1)} all-gather(f32[16,128]{1,0:T(8,128)S(1)} %get-tuple-element.56), channel_id=4, replica_groups={{0,1,64,65},{2,3,66,67},{4,5,68,69},{6,7,70,71},{8,9,72,73},{10,11,74,7..., dimensions={0}, use_global_device_ids=true | all-gather | bytes 40960 | tf_op jit(solution)/shard_map/all_gather | solution.py:268
  45.4 3.2 %collective-permute-start.6 = (f32[8,128]{1,0:T(8,128)S(1)}, f32[8,128]{1,0:T(8,128)S(1)}, u32[]{:S(2)}, u32[]{:S(2)}) collective-permute-start(f32[8,128]{1,0:T(8,128)S(1)} %get-tuple-element.58), channel_id=1, source_target_pairs={{1,2},{2,1},{3,4},{4,3},{5,6},{6,5},{7,8},{8,7},{9,10},{10,9},{11,... | collective-permute-start | bytes 12296 | tf_op jit(solution)/shard_map/ppermute | solution.py:267
  49.2 8.0 %all-gather.3 = f32[64,128]{1,0:T(8,128)S(1)} all-gather(f32[16,128]{1,0:T(8,128)S(1)} %get-tuple-element.60), channel_id=5, replica_groups={{0,1,64,65},{2,3,66,67},{4,5,68,69},{6,7,70,71},{8,9,72,73},{10,11,74,7..., dimensions={0}, use_global_device_ids=true | all-gather | bytes 40960 | tf_op jit(solution)/shard_map/all_gather | solution.py:268
  57.7 4.0 %collective-permute-start.8 = (f32[8,128]{1,0:T(8,128)S(1)}, f32[8,128]{1,0:T(8,128)S(1)}, u32[]{:S(2)}, u32[]{:S(2)}) collective-permute-start(f32[8,128]{1,0:T(8,128)S(1)} %get-tuple-element.62), channel_id=1, source_target_pairs={{1,2},{2,1},{3,4},{4,3},{5,6},{6,5},{7,8},{8,7},{9,10},{10,9},{11,... | collective-permute-start | bytes 12296 | tf_op jit(solution)/shard_map/ppermute | solution.py:267
  62.4 8.2 %all-gather.4 = f32[64,128]{1,0:T(8,128)S(1)} all-gather(f32[16,128]{1,0:T(8,128)S(1)} %get-tuple-element.64), channel_id=6, replica_groups={{0,1,64,65},{2,3,66,67},{4,5,68,69},{6,7,70,71},{8,9,72,73},{10,11,74,7..., dimensions={0}, use_global_device_ids=true | all-gather | bytes 40960 | tf_op jit(solution)/shard_map/all_gather | solution.py:268
  71.1 3.1 %collective-permute-start.10 = (f32[8,128]{1,0:T(8,128)S(1)}, f32[8,128]{1,0:T(8,128)S(1)}, u32[]{:S(2)}, u32[]{:S(2)}) collective-permute-start(f32[8,128]{1,0:T(8,128)S(1)} %get-tuple-element.66), channel_id=1, source_target_pairs={{1,2},{2,1},{3,4},{4,3},{5,6},{6,5},{7,8},{8,7},{9,10},{10,9},{11,... | collective-permute-start | bytes 12296 | tf_op jit(solution)/shard_map/ppermute | solution.py:267
  74.9 7.7 %all-gather.5 = f32[64,128]{1,0:T(8,128)S(1)} all-gather(f32[16,128]{1,0:T(8,128)S(1)} %get-tuple-element.68), channel_id=7, replica_groups={{0,1,64,65},{2,3,66,67},{4,5,68,69},{6,7,70,71},{8,9,72,73},{10,11,74,7..., dimensions={0}, use_global_device_ids=true | all-gather | bytes 40960 | tf_op jit(solution)/shard_map/all_gather | solution.py:268
  83.1 3.6 %collective-permute-start.12 = (f32[8,128]{1,0:T(8,128)S(1)}, f32[8,128]{1,0:T(8,128)S(1)}, u32[]{:S(2)}, u32[]{:S(2)}) collective-permute-start(f32[8,128]{1,0:T(8,128)S(1)} %get-tuple-element.70), channel_id=1, source_target_pairs={{1,2},{2,1},{3,4},{4,3},{5,6},{6,5},{7,8},{8,7},{9,10},{10,9},{11,... | collective-permute-start | bytes 12296 | tf_op jit(solution)/shard_map/ppermute | solution.py:267
  87.4 7.9 %all-gather.6 = f32[64,128]{1,0:T(8,128)S(1)} all-gather(f32[16,128]{1,0:T(8,128)S(1)} %get-tuple-element.72), channel_id=8, replica_groups={{0,1,64,65},{2,3,66,67},{4,5,68,69},{6,7,70,71},{8,9,72,73},{10,11,74,7..., dimensions={0}, use_global_device_ids=true | all-gather | bytes 40960 | tf_op jit(solution)/shard_map/all_gather | solution.py:268
  95.9 3.2 %collective-permute-start.14 = (f32[8,128]{1,0:T(8,128)S(1)}, f32[8,128]{1,0:T(8,128)S(1)}, u32[]{:S(2)}, u32[]{:S(2)}) collective-permute-start(f32[8,128]{1,0:T(8,128)S(1)} %get-tuple-element.74), channel_id=1, source_target_pairs={{1,2},{2,1},{3,4},{4,3},{5,6},{6,5},{7,8},{8,7},{9,10},{10,9},{11,... | collective-permute-start | bytes 12296 | tf_op jit(solution)/shard_map/ppermute | solution.py:267
  99.8 7.5 %all-gather.7 = f32[64,128]{1,0:T(8,128)S(1)} all-gather(f32[16,128]{1,0:T(8,128)S(1)} %get-tuple-element.76), channel_id=9, replica_groups={{0,1,64,65},{2,3,66,67},{4,5,68,69},{6,7,70,71},{8,9,72,73},{10,11,74,7..., dimensions={0}, use_global_device_ids=true | all-gather | bytes 40960 | tf_op jit(solution)/shard_map/all_gather | solution.py:268
  107.8 24.3 %all_to_all.10.sums_ref = f32[64,1,128]{2,1,0:T(1,128)S(1)} all-to-all(f32[64,1,128]{2,1,0:T(1,128)S(1)} %step_7.1), channel_id=1, replica_groups=mesh['slab'=12,'sub_0'=8,'sub_1'=4,'sub_2'=2] {'sub_0','sub_1','sub_2'}, dimensions={0} | all-to-all | bytes 65536 | tf_op jit(solution)/shard_map/all_to_all | solution.py:342
  132.1 0.7 regroup.1
  132.8 8.1 %all-to-all-start.1 = ((f32[12,1,128]{2,1,0:T(1,128)}), f32[12,1,128]{2,1,0:T(1,128)S(1)}, u32[]{:S(2)}, u32[]{:S(2)}) async-start(f32[12,1,128]{2,1,0:T(1,128)} %regroup.1), calls=%async_computation.1 | async-start | bytes 12288 | tf_op jit(solution)/shard_map/all_to_all | solution.py:344
  140.9 2.0 %blocks_out.1.raw_ref = f32[18,26,512]{2,1,0:T(8,128)S(1)} custom-call(f32[9,32,512]{2,1,0:T(8,128)S(1)} %get-tuple-element.42.refs_0_.scaled_ref, s32[32,512]{1,0:T(8,128)S(1)} %get-tuple-element.43.refs_1_.index_ref, f32[24,512]{1,0:T(8,128)S(1)} %get-tuple-element.77.table_ref, s32[4,128]{1,0:T(4,128)S(1)} %pad_add_fusion.refs_3_.side_ref, ...), custom_call_target="tpu_custom_call" | custom-call | tf_op jit(solution)/shard_map/blocks_out/pallas_call | solution.py:228
  143.0 6.8 %all-to-all-done.1.sums_ref = f32[12,1,128]{2,1,0:T(1,128)S(1)} async-done(((f32[12,1,128]{2,1,0:T(1,128)}), f32[12,1,128]{2,1,0:T(1,128)S(1)}, u32[]{:S(2)}, u32[]{:S(2)}) %all-to-all-start.1) | async-done | bytes 6176 | tf_op jit(solution)/shard_map/all_to_all | solution.py:344
  149.8 1.0 finish.1
  (36 shorter events, 9.1 us)
Async XLA Ops:
  2.0 17.3 %collective-permute-start = (f32[24,128]{1,0:T(8,128)S(1)}, f32[24,128]{1,0:T(8,128)S(1)}, u32[]{:S(2)}, u32[]{:S(2)}) collective-permute-start(f32[24,128]{1,0:T(8,128)S(1)} %get-tuple-element.46), channel_id=1, source_target_pairs={{1,2},{2,1},{3,4},{4,3},{5,6},{6,5},{7,8},{8,7},{9,10},{10,9},{11,... | collective-permute-start | bytes 36872 | tf_op jit(solution)/shard_map/ppermute | solution.py:267
  6.5 12.8 %collective-permute-start.1 = (f32[24,128]{1,0:T(8,128)S(1)}, f32[24,128]{1,0:T(8,128)S(1)}, u32[]{:S(2)}, u32[]{:S(2)}) collective-permute-start(f32[24,128]{1,0:T(8,128)S(1)} %get-tuple-element.47), channel_id=1, source_target_pairs={{64,128},{128,64},{192,256},{256,192},{320,384},{384,320},{448,512... | collective-permute-start | bytes 36872 | tf_op jit(solution)/shard_map/ppermute | solution.py:266
  19.8 11.8 %collective-permute-start.2 = (f32[8,128]{1,0:T(8,128)S(1)}, f32[8,128]{1,0:T(8,128)S(1)}, u32[]{:S(2)}, u32[]{:S(2)}) collective-permute-start(f32[8,128]{1,0:T(8,128)S(1)} %get-tuple-element.50), channel_id=1, source_target_pairs={{1,2},{2,1},{3,4},{4,3},{5,6},{6,5},{7,8},{8,7},{9,10},{10,9},{11,... | collective-permute-start | bytes 12296 | tf_op jit(solution)/shard_map/ppermute | solution.py:267
  21.7 9.9 %collective-permute-start.3 = (f32[8,128]{1,0:T(8,128)S(1)}, f32[8,128]{1,0:T(8,128)S(1)}, u32[]{:S(2)}, u32[]{:S(2)}) collective-permute-start(f32[8,128]{1,0:T(8,128)S(1)} %get-tuple-element.51), channel_id=1, source_target_pairs={{64,128},{128,64},{192,256},{256,192},{320,384},{384,320},{448,512... | collective-permute-start | bytes 12296 | tf_op jit(solution)/shard_map/ppermute | solution.py:266
  32.1 12.8 %collective-permute-start.4 = (f32[8,128]{1,0:T(8,128)S(1)}, f32[8,128]{1,0:T(8,128)S(1)}, u32[]{:S(2)}, u32[]{:S(2)}) collective-permute-start(f32[8,128]{1,0:T(8,128)S(1)} %get-tuple-element.54), channel_id=1, source_target_pairs={{1,2},{2,1},{3,4},{4,3},{5,6},{6,5},{7,8},{8,7},{9,10},{10,9},{11,... | collective-permute-start | bytes 12296 | tf_op jit(solution)/shard_map/ppermute | solution.py:267
  35.0 9.9 %collective-permute-start.5 = (f32[8,128]{1,0:T(8,128)S(1)}, f32[8,128]{1,0:T(8,128)S(1)}, u32[]{:S(2)}, u32[]{:S(2)}) collective-permute-start(f32[8,128]{1,0:T(8,128)S(1)} %get-tuple-element.55), channel_id=1, source_target_pairs={{64,128},{128,64},{192,256},{256,192},{320,384},{384,320},{448,512... | collective-permute-start | bytes 12296 | tf_op jit(solution)/shard_map/ppermute | solution.py:266
  45.4 11.9 %collective-permute-start.6 = (f32[8,128]{1,0:T(8,128)S(1)}, f32[8,128]{1,0:T(8,128)S(1)}, u32[]{:S(2)}, u32[]{:S(2)}) collective-permute-start(f32[8,128]{1,0:T(8,128)S(1)} %get-tuple-element.58), channel_id=1, source_target_pairs={{1,2},{2,1},{3,4},{4,3},{5,6},{6,5},{7,8},{8,7},{9,10},{10,9},{11,... | collective-permute-start | bytes 12296 | tf_op jit(solution)/shard_map/ppermute | solution.py:267
  48.6 8.7 %collective-permute-start.7 = (f32[8,128]{1,0:T(8,128)S(1)}, f32[8,128]{1,0:T(8,128)S(1)}, u32[]{:S(2)}, u32[]{:S(2)}) collective-permute-start(f32[8,128]{1,0:T(8,128)S(1)} %get-tuple-element.59), channel_id=1, source_target_pairs={{64,128},{128,64},{192,256},{256,192},{320,384},{384,320},{448,512... | collective-permute-start | bytes 12296 | tf_op jit(solution)/shard_map/ppermute | solution.py:266
  57.7 12.9 %collective-permute-start.8 = (f32[8,128]{1,0:T(8,128)S(1)}, f32[8,128]{1,0:T(8,128)S(1)}, u32[]{:S(2)}, u32[]{:S(2)}) collective-permute-start(f32[8,128]{1,0:T(8,128)S(1)} %get-tuple-element.62), channel_id=1, source_target_pairs={{1,2},{2,1},{3,4},{4,3},{5,6},{6,5},{7,8},{8,7},{9,10},{10,9},{11,... | collective-permute-start | bytes 12296 | tf_op jit(solution)/shard_map/ppermute | solution.py:267
  61.8 8.9 %collective-permute-start.9 = (f32[8,128]{1,0:T(8,128)S(1)}, f32[8,128]{1,0:T(8,128)S(1)}, u32[]{:S(2)}, u32[]{:S(2)}) collective-permute-start(f32[8,128]{1,0:T(8,128)S(1)} %get-tuple-element.63), channel_id=1, source_target_pairs={{64,128},{128,64},{192,256},{256,192},{320,384},{384,320},{448,512... | collective-permute-start | bytes 12296 | tf_op jit(solution)/shard_map/ppermute | solution.py:266
  71.1 11.4 %collective-permute-start.10 = (f32[8,128]{1,0:T(8,128)S(1)}, f32[8,128]{1,0:T(8,128)S(1)}, u32[]{:S(2)}, u32[]{:S(2)}) collective-permute-start(f32[8,128]{1,0:T(8,128)S(1)} %get-tuple-element.66), channel_id=1, source_target_pairs={{1,2},{2,1},{3,4},{4,3},{5,6},{6,5},{7,8},{8,7},{9,10},{10,9},{11,... | collective-permute-start | bytes 12296 | tf_op jit(solution)/shard_map/ppermute | solution.py:267
  74.2 8.4 %collective-permute-start.11 = (f32[8,128]{1,0:T(8,128)S(1)}, f32[8,128]{1,0:T(8,128)S(1)}, u32[]{:S(2)}, u32[]{:S(2)}) collective-permute-start(f32[8,128]{1,0:T(8,128)S(1)} %get-tuple-element.67), channel_id=1, source_target_pairs={{64,128},{128,64},{192,256},{256,192},{320,384},{384,320},{448,512... | collective-permute-start | bytes 12296 | tf_op jit(solution)/shard_map/ppermute | solution.py:266
  83.1 12.3 %collective-permute-start.12 = (f32[8,128]{1,0:T(8,128)S(1)}, f32[8,128]{1,0:T(8,128)S(1)}, u32[]{:S(2)}, u32[]{:S(2)}) collective-permute-start(f32[8,128]{1,0:T(8,128)S(1)} %get-tuple-element.70), channel_id=1, source_target_pairs={{1,2},{2,1},{3,4},{4,3},{5,6},{6,5},{7,8},{8,7},{9,10},{10,9},{11,... | collective-permute-start | bytes 12296 | tf_op jit(solution)/shard_map/ppermute | solution.py:267
  86.7 8.6 %collective-permute-start.13 = (f32[8,128]{1,0:T(8,128)S(1)}, f32[8,128]{1,0:T(8,128)S(1)}, u32[]{:S(2)}, u32[]{:S(2)}) collective-permute-start(f32[8,128]{1,0:T(8,128)S(1)} %get-tuple-element.71), channel_id=1, source_target_pairs={{64,128},{128,64},{192,256},{256,192},{320,384},{384,320},{448,512... | collective-permute-start | bytes 12296 | tf_op jit(solution)/shard_map/ppermute | solution.py:266
  95.9 11.4 %collective-permute-start.14 = (f32[8,128]{1,0:T(8,128)S(1)}, f32[8,128]{1,0:T(8,128)S(1)}, u32[]{:S(2)}, u32[]{:S(2)}) collective-permute-start(f32[8,128]{1,0:T(8,128)S(1)} %get-tuple-element.74), channel_id=1, source_target_pairs={{1,2},{2,1},{3,4},{4,3},{5,6},{6,5},{7,8},{8,7},{9,10},{10,9},{11,... | collective-permute-start | bytes 12296 | tf_op jit(solution)/shard_map/ppermute | solution.py:267
  99.1 8.2 %collective-permute-start.15 = (f32[8,128]{1,0:T(8,128)S(1)}, f32[8,128]{1,0:T(8,128)S(1)}, u32[]{:S(2)}, u32[]{:S(2)}) collective-permute-start(f32[8,128]{1,0:T(8,128)S(1)} %get-tuple-element.75), channel_id=1, source_target_pairs={{64,128},{128,64},{192,256},{256,192},{320,384},{384,320},{448,512... | collective-permute-start | bytes 12296 | tf_op jit(solution)/shard_map/ppermute | solution.py:266
  132.8 17.0 %all-to-all-start.1 = ((f32[12,1,128]{2,1,0:T(1,128)}), f32[12,1,128]{2,1,0:T(1,128)S(1)}, u32[]{:S(2)}, u32[]{:S(2)}) async-start(f32[12,1,128]{2,1,0:T(1,128)} %regroup.1), calls=%async_computation.1 | async-start | bytes 12288 | tf_op jit(solution)/shard_map/all_to_all | solution.py:344

commit v3 on v2

--- a/solution.py
+++ b/solution.py
@@ -11,6 +11,8 @@
 ITERS = 8
 OMEGA = 4.0 / 3.0
 SUB = ("sub_0", "sub_1", "sub_2")
+FIRST = ("slab", "sub_2")
+SECOND = ("sub_0", "sub_1")
 SLAB_SUB = ("slab", "sub_0", "sub_1", "sub_2")
 LANES = 128
 F32 = jnp.float32
@@ -43,8 +45,11 @@
             rows = slice(tile * 8, tile * 8 + 8)
             sources = [table_ref[rows, lanes(group)] for group in range(4)]
             pay_ref[rows, :] = pick(sources, low, high)
-    both_ref[0 : tiles * 8, :] = pay_refs[0][...]
-    both_ref[tiles * 8 :, :] = pay_refs[1][...]
+    rows = 3 if tiles == 1 else tiles * 8
+    if tiles == 1:
+        both_ref[...] = jnp.zeros(both_ref.shape, F32)
+    both_ref[0:rows, :] = pay_refs[0][0:rows, :]
+    both_ref[rows : 2 * rows, :] = pay_refs[1][0:rows, :]
 
 
 def start_kernel(*refs):
@@ -112,7 +117,7 @@
     ao, bo, gathered = refs
     odd_sub = side_ref[2:3, :] != 0
     odd_slab = side_ref[3:4, :] != 0
-    half = gathered.shape[1] // 2
+    half = 3 if gathered.shape[1] == 8 else gathered.shape[1] // 2
     down = slice(row.start + half, row.stop + half)
     even_a = jnp.where(
         odd_slab,
@@ -310,9 +315,9 @@
     first_received = received
     for iteration in range(ITERS):
         last = iteration == ITERS - 1
-        outs = [kept_f32(8, nodes)] + [kept_f32(8, LANES)] * 2 + [kept_f32(16, LANES)]
+        outs = [kept_f32(8, nodes)] + [kept_f32(8, LANES)] * 3
         if last:
-            outs = [kept_f32(subs, 1, LANES)]
+            outs = [kept_f32(lax.axis_size(FIRST), 1, LANES)]
         result = call(
             functools.partial(step_kernel, iteration == 0, last),
             f"step_{iteration}",
@@ -339,9 +344,9 @@
         side,
         *first_received,
     )
-    sums = lax.all_to_all(sums, SUB, 0, 0, tiled=True)
-    (sums,) = call(regroup_kernel, "regroup", [kept_f32(slabs, 1, LANES)], kept(sums))
-    sums = lax.all_to_all(sums, "slab", 0, 0, tiled=True)
+    sums = lax.all_to_all(sums, FIRST, 0, 0, tiled=True)
+    (sums,) = call(regroup_kernel, "regroup", [kept_f32(lax.axis_size(SECOND), 1, LANES)], kept(sums))
+    sums = lax.all_to_all(sums, SECOND, 0, 0, tiled=True)
     prolong_off, prolong_self, rho = call(
         finish_kernel,
         "finish",

time: 151 us -> 151 us (level)
  starting transfers between devices: 39.8 us -> 48.2 us
  blocking collectives: 93.8 us -> 85.5 us
    all_to_all x1, blocking collectives: 24.3 us -> 15.9 us  [body(): sums = lax.all_to_all(sums, FIRST, 0, 0, tiled=True)]
    all_to_all x1, starting transfers between devices: 8.14 us -> 16.4 us  [body(): sums = lax.all_to_all(sums, SECOND, 0, 0, tiled=True)]
where the time goes in v3:
time: 151 us; the launch traced here: 150 us
  blocking collectives  85.5 us (57%)
  starting transfers between devices  48.2 us (32%)
  Pallas kernels  9.19 us (6%)
  waiting for transfers between devices  6.54 us (4%)
    all_gather x8, blocking collectives, exchange(): return (ao, bo, lax.all_gather(both, SLAB_SUB, axis_index_groups=squares()))  69.6 us
    ppermute x8, starting transfers between devices, exchange(): ao = lax.ppermute(a, SUB, swap(lax.axis_size(SUB), 1))  26.4 us
    all_to_all x1, starting transfers between devices, body(): sums = lax.all_to_all(sums, SECOND, 0, 0, tiled=True)  16.4 us
    all_to_all x1, blocking collectives, body(): sums = lax.all_to_all(sums, FIRST, 0, 0, tiled=True)  15.9 us
    pallas_call x12, Pallas kernels, call(): pl.pallas_call(kernel, name=name, out_shape=[jax.ShapeDtypeStruct(*out) i...  9.19 us
    all_to_all x1, waiting for transfers between devices, body(): sums = lax.all_to_all(sums, SECOND, 0, 0, tiled=True)  6.5 us
    ppermute x8, starting transfers between devices, exchange(): bo = lax.ppermute(b, 'slab', swap(lax.axis_size('slab'), 1))  5.29 us
  transfers between devices with their start and end apart: 17, of which 1 were waited for; matrix products, arithmetic and copies ran while one was open for 0% of the time, Pallas kernels for 1%

profile of v3, /device:TPU:1, one launch (start us, length us, event | category | flops | bytes accessed | tf_op | source)
XLA Modules:
  0.0 150.5 jit_solution(247887131482412147)
XLA Ops:
  0.6 1.4 start.1
  2.0 4.5 %collective-permute-start = (f32[24,128]{1,0:T(8,128)S(1)}, f32[24,128]{1,0:T(8,128)S(1)}, u32[]{:S(2)}, u32[]{:S(2)}) collective-permute-start(f32[24,128]{1,0:T(8,128)S(1)} %get-tuple-element.46), channel_id=1, source_target_pairs={{1,2},{2,1},{3,4},{4,3},{5,6},{6,5},{7,8},{8,7},{9,10},{10,9},{11,... | collective-permute-start | bytes 36872 | tf_op jit(solution)/shard_map/ppermute | solution.py:272
  6.5 0.7 collective-permute-start.1
  7.5 11.8 %all-gather = f32[192,128]{1,0:T(8,128)S(1)} all-gather(f32[48,128]{1,0:T(8,128)S(1)} %get-tuple-element.48), channel_id=2, replica_groups={{0,1,64,65},{2,3,66,67},{4,5,68,69},{6,7,70,71},{8,9,72,73},{10,11,74,7..., dimensions={0}, use_global_device_ids=true | all-gather | bytes 122880 | tf_op jit(solution)/shard_map/all_gather | solution.py:273
  19.8 1.9 %collective-permute-start.2 = (f32[8,128]{1,0:T(8,128)S(1)}, f32[8,128]{1,0:T(8,128)S(1)}, u32[]{:S(2)}, u32[]{:S(2)}) collective-permute-start(f32[8,128]{1,0:T(8,128)S(1)} %get-tuple-element.50), channel_id=1, source_target_pairs={{1,2},{2,1},{3,4},{4,3},{5,6},{6,5},{7,8},{8,7},{9,10},{10,9},{11,... | collective-permute-start | bytes 12296 | tf_op jit(solution)/shard_map/ppermute | solution.py:272
  21.7 0.7 collective-permute-start.3
  22.4 9.2 %all-gather.1 = f32[32,128]{1,0:T(8,128)S(1)} all-gather(f32[8,128]{1,0:T(8,128)S(1)} %get-tuple-element.52), channel_id=3, replica_groups={{0,1,64,65},{2,3,66,67},{4,5,68,69},{6,7,70,71},{8,9,72,73},{10,11,74,7..., dimensions={0}, use_global_device_ids=true | all-gather | bytes 20480 | tf_op jit(solution)/shard_map/all_gather | solution.py:273
  32.1 2.9 %collective-permute-start.4 = (f32[8,128]{1,0:T(8,128)S(1)}, f32[8,128]{1,0:T(8,128)S(1)}, u32[]{:S(2)}, u32[]{:S(2)}) collective-permute-start(f32[8,128]{1,0:T(8,128)S(1)} %get-tuple-element.54), channel_id=1, source_target_pairs={{1,2},{2,1},{3,4},{4,3},{5,6},{6,5},{7,8},{8,7},{9,10},{10,9},{11,... | collective-permute-start | bytes 12296 | tf_op jit(solution)/shard_map/ppermute | solution.py:272
  35.7 9.2 %all-gather.2 = f32[32,128]{1,0:T(8,128)S(1)} all-gather(f32[8,128]{1,0:T(8,128)S(1)} %get-tuple-element.56), channel_id=4, replica_groups={{0,1,64,65},{2,3,66,67},{4,5,68,69},{6,7,70,71},{8,9,72,73},{10,11,74,7..., dimensions={0}, use_global_device_ids=true | all-gather | bytes 20480 | tf_op jit(solution)/shard_map/all_gather | solution.py:273
  45.4 3.2 %collective-permute-start.6 = (f32[8,128]{1,0:T(8,128)S(1)}, f32[8,128]{1,0:T(8,128)S(1)}, u32[]{:S(2)}, u32[]{:S(2)}) collective-permute-start(f32[8,128]{1,0:T(8,128)S(1)} %get-tuple-element.58), channel_id=1, source_target_pairs={{1,2},{2,1},{3,4},{4,3},{5,6},{6,5},{7,8},{8,7},{9,10},{10,9},{11,... | collective-permute-start | bytes 12296 | tf_op jit(solution)/shard_map/ppermute | solution.py:272
  49.3 8.0 %all-gather.3 = f32[32,128]{1,0:T(8,128)S(1)} all-gather(f32[8,128]{1,0:T(8,128)S(1)} %get-tuple-element.60), channel_id=5, replica_groups={{0,1,64,65},{2,3,66,67},{4,5,68,69},{6,7,70,71},{8,9,72,73},{10,11,74,7..., dimensions={0}, use_global_device_ids=true | all-gather | bytes 20480 | tf_op jit(solution)/shard_map/all_gather | solution.py:273
  57.8 4.0 %collective-permute-start.8 = (f32[8,128]{1,0:T(8,128)S(1)}, f32[8,128]{1,0:T(8,128)S(1)}, u32[]{:S(2)}, u32[]{:S(2)}) collective-permute-start(f32[8,128]{1,0:T(8,128)S(1)} %get-tuple-element.62), channel_id=1, source_target_pairs={{1,2},{2,1},{3,4},{4,3},{5,6},{6,5},{7,8},{8,7},{9,10},{10,9},{11,... | collective-permute-start | bytes 12296 | tf_op jit(solution)/shard_map/ppermute | solution.py:272
  62.5 8.2 %all-gather.4 = f32[32,128]{1,0:T(8,128)S(1)} all-gather(f32[8,128]{1,0:T(8,128)S(1)} %get-tuple-element.64), channel_id=6, replica_groups={{0,1,64,65},{2,3,66,67},{4,5,68,69},{6,7,70,71},{8,9,72,73},{10,11,74,7..., dimensions={0}, use_global_device_ids=true | all-gather | bytes 20480 | tf_op jit(solution)/shard_map/all_gather | solution.py:273
  71.2 3.1 %collective-permute-start.10 = (f32[8,128]{1,0:T(8,128)S(1)}, f32[8,128]{1,0:T(8,128)S(1)}, u32[]{:S(2)}, u32[]{:S(2)}) collective-permute-start(f32[8,128]{1,0:T(8,128)S(1)} %get-tuple-element.66), channel_id=1, source_target_pairs={{1,2},{2,1},{3,4},{4,3},{5,6},{6,5},{7,8},{8,7},{9,10},{10,9},{11,... | collective-permute-start | bytes 12296 | tf_op jit(solution)/shard_map/ppermute | solution.py:272
  75.0 7.7 %all-gather.5 = f32[32,128]{1,0:T(8,128)S(1)} all-gather(f32[8,128]{1,0:T(8,128)S(1)} %get-tuple-element.68), channel_id=7, replica_groups={{0,1,64,65},{2,3,66,67},{4,5,68,69},{6,7,70,71},{8,9,72,73},{10,11,74,7..., dimensions={0}, use_global_device_ids=true | all-gather | bytes 20480 | tf_op jit(solution)/shard_map/all_gather | solution.py:273
  83.2 3.6 %collective-permute-start.12 = (f32[8,128]{1,0:T(8,128)S(1)}, f32[8,128]{1,0:T(8,128)S(1)}, u32[]{:S(2)}, u32[]{:S(2)}) collective-permute-start(f32[8,128]{1,0:T(8,128)S(1)} %get-tuple-element.70), channel_id=1, source_target_pairs={{1,2},{2,1},{3,4},{4,3},{5,6},{6,5},{7,8},{8,7},{9,10},{10,9},{11,... | collective-permute-start | bytes 12296 | tf_op jit(solution)/shard_map/ppermute | solution.py:272
  87.5 8.0 %all-gather.6 = f32[32,128]{1,0:T(8,128)S(1)} all-gather(f32[8,128]{1,0:T(8,128)S(1)} %get-tuple-element.72), channel_id=8, replica_groups={{0,1,64,65},{2,3,66,67},{4,5,68,69},{6,7,70,71},{8,9,72,73},{10,11,74,7..., dimensions={0}, use_global_device_ids=true | all-gather | bytes 20480 | tf_op jit(solution)/shard_map/all_gather | solution.py:273
  96.0 3.3 %collective-permute-start.14 = (f32[8,128]{1,0:T(8,128)S(1)}, f32[8,128]{1,0:T(8,128)S(1)}, u32[]{:S(2)}, u32[]{:S(2)}) collective-permute-start(f32[8,128]{1,0:T(8,128)S(1)} %get-tuple-element.74), channel_id=1, source_target_pairs={{1,2},{2,1},{3,4},{4,3},{5,6},{6,5},{7,8},{8,7},{9,10},{10,9},{11,... | collective-permute-start | bytes 12296 | tf_op jit(solution)/shard_map/ppermute | solution.py:272
  99.9 7.5 %all-gather.7 = f32[32,128]{1,0:T(8,128)S(1)} all-gather(f32[8,128]{1,0:T(8,128)S(1)} %get-tuple-element.76), channel_id=9, replica_groups={{0,1,64,65},{2,3,66,67},{4,5,68,69},{6,7,70,71},{8,9,72,73},{10,11,74,7..., dimensions={0}, use_global_device_ids=true | all-gather | bytes 20480 | tf_op jit(solution)/shard_map/all_gather | solution.py:273
  108.0 15.9 %all_to_all.10.sums_ref = f32[24,1,128]{2,1,0:T(1,128)S(1)} all-to-all(f32[24,1,128]{2,1,0:T(1,128)S(1)} %step_7.1), channel_id=1, replica_groups=mesh['slab'=12,'sub_0'=8,'sub_1'=4,'sub_2'=2] {'slab','sub_2'}, dimensions={0} | all-to-all | bytes 24576 | tf_op jit(solution)/shard_map/all_to_all | solution.py:347
  124.5 16.4 %all-to-all-start.1 = ((f32[32,1,128]{2,1,0:T(1,128)}), f32[32,1,128]{2,1,0:T(1,128)S(1)}, u32[]{:S(2)}, u32[]{:S(2)}) async-start(f32[32,1,128]{2,1,0:T(1,128)} %regroup.1), calls=%async_computation.1 | async-start | bytes 32768 | tf_op jit(solution)/shard_map/all_to_all | solution.py:349
  140.9 2.0 %blocks_out.1.raw_ref = f32[18,26,512]{2,1,0:T(8,128)S(1)} custom-call(f32[9,32,512]{2,1,0:T(8,128)S(1)} %get-tuple-element.42.refs_0_.scaled_ref, s32[32,512]{1,0:T(8,128)S(1)} %get-tuple-element.43.refs_1_.index_ref, f32[24,512]{1,0:T(8,128)S(1)} %get-tuple-element.77.table_ref, s32[4,128]{1,0:T(4,128)S(1)} %pad_add_fusion.refs_3_.side_ref, ...), custom_call_target="tpu_custom_call" | custom-call | tf_op jit(solution)/shard_map/blocks_out/pallas_call | solution.py:233
  143.0 6.5 %all-to-all-done.1.sums_ref = f32[32,1,128]{2,1,0:T(1,128)S(1)} async-done(((f32[32,1,128]{2,1,0:T(1,128)}), f32[32,1,128]{2,1,0:T(1,128)S(1)}, u32[]{:S(2)}, u32[]{:S(2)}) %all-to-all-start.1) | async-done | bytes 16416 | tf_op jit(solution)/shard_map/all_to_all | solution.py:349
  149.5 1.0 finish.1
  (36 shorter events, 9.1 us)
Async XLA Ops:
  2.0 17.3 %collective-permute-start = (f32[24,128]{1,0:T(8,128)S(1)}, f32[24,128]{1,0:T(8,128)S(1)}, u32[]{:S(2)}, u32[]{:S(2)}) collective-permute-start(f32[24,128]{1,0:T(8,128)S(1)} %get-tuple-element.46), channel_id=1, source_target_pairs={{1,2},{2,1},{3,4},{4,3},{5,6},{6,5},{7,8},{8,7},{9,10},{10,9},{11,... | collective-permute-start | bytes 36872 | tf_op jit(solution)/shard_map/ppermute | solution.py:272
  6.5 12.8 %collective-permute-start.1 = (f32[24,128]{1,0:T(8,128)S(1)}, f32[24,128]{1,0:T(8,128)S(1)}, u32[]{:S(2)}, u32[]{:S(2)}) collective-permute-start(f32[24,128]{1,0:T(8,128)S(1)} %get-tuple-element.47), channel_id=1, source_target_pairs={{64,128},{128,64},{192,256},{256,192},{320,384},{384,320},{448,512... | collective-permute-start | bytes 36872 | tf_op jit(solution)/shard_map/ppermute | solution.py:271
  19.8 11.8 %collective-permute-start.2 = (f32[8,128]{1,0:T(8,128)S(1)}, f32[8,128]{1,0:T(8,128)S(1)}, u32[]{:S(2)}, u32[]{:S(2)}) collective-permute-start(f32[8,128]{1,0:T(8,128)S(1)} %get-tuple-element.50), channel_id=1, source_target_pairs={{1,2},{2,1},{3,4},{4,3},{5,6},{6,5},{7,8},{8,7},{9,10},{10,9},{11,... | collective-permute-start | bytes 12296 | tf_op jit(solution)/shard_map/ppermute | solution.py:272
  21.7 9.9 %collective-permute-start.3 = (f32[8,128]{1,0:T(8,128)S(1)}, f32[8,128]{1,0:T(8,128)S(1)}, u32[]{:S(2)}, u32[]{:S(2)}) collective-permute-start(f32[8,128]{1,0:T(8,128)S(1)} %get-tuple-element.51), channel_id=1, source_target_pairs={{64,128},{128,64},{192,256},{256,192},{320,384},{384,320},{448,512... | collective-permute-start | bytes 12296 | tf_op jit(solution)/shard_map/ppermute | solution.py:271
  32.1 12.8 %collective-permute-start.4 = (f32[8,128]{1,0:T(8,128)S(1)}, f32[8,128]{1,0:T(8,128)S(1)}, u32[]{:S(2)}, u32[]{:S(2)}) collective-permute-start(f32[8,128]{1,0:T(8,128)S(1)} %get-tuple-element.54), channel_id=1, source_target_pairs={{1,2},{2,1},{3,4},{4,3},{5,6},{6,5},{7,8},{8,7},{9,10},{10,9},{11,... | collective-permute-start | bytes 12296 | tf_op jit(solution)/shard_map/ppermute | solution.py:272
  35.0 9.9 %collective-permute-start.5 = (f32[8,128]{1,0:T(8,128)S(1)}, f32[8,128]{1,0:T(8,128)S(1)}, u32[]{:S(2)}, u32[]{:S(2)}) collective-permute-start(f32[8,128]{1,0:T(8,128)S(1)} %get-tuple-element.55), channel_id=1, source_target_pairs={{64,128},{128,64},{192,256},{256,192},{320,384},{384,320},{448,512... | collective-permute-start | bytes 12296 | tf_op jit(solution)/shard_map/ppermute | solution.py:271
  45.4 11.9 %collective-permute-start.6 = (f32[8,128]{1,0:T(8,128)S(1)}, f32[8,128]{1,0:T(8,128)S(1)}, u32[]{:S(2)}, u32[]{:S(2)}) collective-permute-start(f32[8,128]{1,0:T(8,128)S(1)} %get-tuple-element.58), channel_id=1, source_target_pairs={{1,2},{2,1},{3,4},{4,3},{5,6},{6,5},{7,8},{8,7},{9,10},{10,9},{11,... | collective-permute-start | bytes 12296 | tf_op jit(solution)/shard_map/ppermute | solution.py:272
  48.6 8.7 %collective-permute-start.7 = (f32[8,128]{1,0:T(8,128)S(1)}, f32[8,128]{1,0:T(8,128)S(1)}, u32[]{:S(2)}, u32[]{:S(2)}) collective-permute-start(f32[8,128]{1,0:T(8,128)S(1)} %get-tuple-element.59), channel_id=1, source_target_pairs={{64,128},{128,64},{192,256},{256,192},{320,384},{384,320},{448,512... | collective-permute-start | bytes 12296 | tf_op jit(solution)/shard_map/ppermute | solution.py:271
  57.8 12.9 %collective-permute-start.8 = (f32[8,128]{1,0:T(8,128)S(1)}, f32[8,128]{1,0:T(8,128)S(1)}, u32[]{:S(2)}, u32[]{:S(2)}) collective-permute-start(f32[8,128]{1,0:T(8,128)S(1)} %get-tuple-element.62), channel_id=1, source_target_pairs={{1,2},{2,1},{3,4},{4,3},{5,6},{6,5},{7,8},{8,7},{9,10},{10,9},{11,... | collective-permute-start | bytes 12296 | tf_op jit(solution)/shard_map/ppermute | solution.py:272
  61.8 8.9 %collective-permute-start.9 = (f32[8,128]{1,0:T(8,128)S(1)}, f32[8,128]{1,0:T(8,128)S(1)}, u32[]{:S(2)}, u32[]{:S(2)}) collective-permute-start(f32[8,128]{1,0:T(8,128)S(1)} %get-tuple-element.63), channel_id=1, source_target_pairs={{64,128},{128,64},{192,256},{256,192},{320,384},{384,320},{448,512... | collective-permute-start | bytes 12296 | tf_op jit(solution)/shard_map/ppermute | solution.py:271
  71.2 11.5 %collective-permute-start.10 = (f32[8,128]{1,0:T(8,128)S(1)}, f32[8,128]{1,0:T(8,128)S(1)}, u32[]{:S(2)}, u32[]{:S(2)}) collective-permute-start(f32[8,128]{1,0:T(8,128)S(1)} %get-tuple-element.66), channel_id=1, source_target_pairs={{1,2},{2,1},{3,4},{4,3},{5,6},{6,5},{7,8},{8,7},{9,10},{10,9},{11,... | collective-permute-start | bytes 12296 | tf_op jit(solution)/shard_map/ppermute | solution.py:272
  74.3 8.4 %collective-permute-start.11 = (f32[8,128]{1,0:T(8,128)S(1)}, f32[8,128]{1,0:T(8,128)S(1)}, u32[]{:S(2)}, u32[]{:S(2)}) collective-permute-start(f32[8,128]{1,0:T(8,128)S(1)} %get-tuple-element.67), channel_id=1, source_target_pairs={{64,128},{128,64},{192,256},{256,192},{320,384},{384,320},{448,512... | collective-permute-start | bytes 12296 | tf_op jit(solution)/shard_map/ppermute | solution.py:271
  83.2 12.3 %collective-permute-start.12 = (f32[8,128]{1,0:T(8,128)S(1)}, f32[8,128]{1,0:T(8,128)S(1)}, u32[]{:S(2)}, u32[]{:S(2)}) collective-permute-start(f32[8,128]{1,0:T(8,128)S(1)} %get-tuple-element.70), channel_id=1, source_target_pairs={{1,2},{2,1},{3,4},{4,3},{5,6},{6,5},{7,8},{8,7},{9,10},{10,9},{11,... | collective-permute-start | bytes 12296 | tf_op jit(solution)/shard_map/ppermute | solution.py:272
  86.8 8.6 %collective-permute-start.13 = (f32[8,128]{1,0:T(8,128)S(1)}, f32[8,128]{1,0:T(8,128)S(1)}, u32[]{:S(2)}, u32[]{:S(2)}) collective-permute-start(f32[8,128]{1,0:T(8,128)S(1)} %get-tuple-element.71), channel_id=1, source_target_pairs={{64,128},{128,64},{192,256},{256,192},{320,384},{384,320},{448,512... | collective-permute-start | bytes 12296 | tf_op jit(solution)/shard_map/ppermute | solution.py:271
  96.0 11.5 %collective-permute-start.14 = (f32[8,128]{1,0:T(8,128)S(1)}, f32[8,128]{1,0:T(8,128)S(1)}, u32[]{:S(2)}, u32[]{:S(2)}) collective-permute-start(f32[8,128]{1,0:T(8,128)S(1)} %get-tuple-element.74), channel_id=1, source_target_pairs={{1,2},{2,1},{3,4},{4,3},{5,6},{6,5},{7,8},{8,7},{9,10},{10,9},{11,... | collective-permute-start | bytes 12296 | tf_op jit(solution)/shard_map/ppermute | solution.py:272
  99.3 8.2 %collective-permute-start.15 = (f32[8,128]{1,0:T(8,128)S(1)}, f32[8,128]{1,0:T(8,128)S(1)}, u32[]{:S(2)}, u32[]{:S(2)}) collective-permute-start(f32[8,128]{1,0:T(8,128)S(1)} %get-tuple-element.75), channel_id=1, source_target_pairs={{64,128},{128,64},{192,256},{256,192},{320,384},{384,320},{448,512... | collective-permute-start | bytes 12296 | tf_op jit(solution)/shard_map/ppermute | solution.py:271
  124.5 25.0 %all-to-all-start.1 = ((f32[32,1,128]{2,1,0:T(1,128)}), f32[32,1,128]{2,1,0:T(1,128)S(1)}, u32[]{:S(2)}, u32[]{:S(2)}) async-start(f32[32,1,128]{2,1,0:T(1,128)} %regroup.1), calls=%async_computation.1 | async-start | bytes 32768 | tf_op jit(solution)/shard_map/all_to_all | solution.py:349

commit v4 on v3

--- a/solution.py
+++ b/solution.py
@@ -54,8 +54,8 @@
 
 def start_kernel(*refs):
     far_refs, refs = refs[:7], refs[7:]
-    table_ref, w_ref, send_ref, a_ref, b_ref, both_ref, scaled_ref, index_ref = refs[:8]
-    near_refs, sems = refs[8:15], refs[15:]
+    table_ref, w_ref, send_ref, a_ref, b_ref, both_ref, scaled_ref, index_ref, side_ref = refs[:9]
+    near_refs, sems = refs[9:16], refs[16:]
     copies = [
         pltpu.make_async_copy(source, target, sem)
         for source, target, sem in zip(far_refs, near_refs, sems)
@@ -63,6 +63,12 @@
     for copy in copies:
         copy.start()
     near_ref, aggregates_ref, start_ref, sends_ref, diag_ref, off_ref, columns_ref = near_refs
+    lane = lax.broadcasted_iota(jnp.int32, (1, LANES), 1)
+    low_half = (lane < 64).astype(jnp.int32)
+    for row, axis in enumerate((SUB, "slab")):
+        odd = (lane * 0 + lax.axis_index(axis)) & 1
+        side_ref[row : row + 1, :] = low_half ^ odd
+        side_ref[row + 2 : row + 3, :] = odd
     for copy in copies[:4]:
         copy.wait()
     nodes = near_ref.shape[1]
@@ -278,19 +284,15 @@
     slots = off_blocks.shape[0]
     padded = (slots + 7) // 8 * 8
     subs, slabs = lax.axis_size(SUB), lax.axis_size("slab")
-    lane = jnp.arange(LANES, dtype=jnp.int32)[None, :]
-    position = jnp.stack([lax.axis_index(SUB), lax.axis_index("slab")])[:, None] % 2
-    side = ((lane < 64) == (position == 0)).astype(jnp.int32)
-    side = jnp.concatenate([side, jnp.broadcast_to(position, side.shape)]).astype(jnp.int32)
-
     kept_f32 = lambda *shape: (shape, F32, "kept")
     kept_i32 = lambda *shape: (shape, jnp.int32, "kept")
-    table, w, send, a, b, both, scaled, index = call(
+    table, w, send, a, b, both, scaled, index, side = call(
         start_kernel,
         "start",
         [kept_f32(24, nodes), kept_f32(8, nodes), kept_i32(2, LANES)]
         + [kept_f32(24, LANES)] * 2
-        + [kept_f32(48, LANES), kept_f32(9, padded, nodes), kept_i32(padded, nodes)],
+        + [kept_f32(48, LANES), kept_f32(9, padded, nodes), kept_i32(padded, nodes)]
+        + [kept_i32(4, LANES)],
         far(near_null),
         far(aggregates[None, :]),
         far(start_vector),

time: 151 us -> 151 us (level)
  no operation moved by 1% of the time
where the time goes in v4:
time: 151 us; the launch traced here: 150 us
  blocking collectives  85.5 us (57%)
  starting transfers between devices  48.2 us (32%)
  Pallas kernels  9.12 us (6%)
  waiting for transfers between devices  6.61 us (4%)
    all_gather x8, blocking collectives, exchange(): return (ao, bo, lax.all_gather(both, SLAB_SUB, axis_index_groups=squares()))  69.6 us
    ppermute x8, starting transfers between devices, exchange(): ao = lax.ppermute(a, SUB, swap(lax.axis_size(SUB), 1))  26.4 us
    all_to_all x1, starting transfers between devices, body(): sums = lax.all_to_all(sums, SECOND, 0, 0, tiled=True)  16.4 us
    all_to_all x1, blocking collectives, body(): sums = lax.all_to_all(sums, FIRST, 0, 0, tiled=True)  15.9 us
    pallas_call x12, Pallas kernels, call(): pl.pallas_call(kernel, name=name, out_shape=[jax.ShapeDtypeStruct(*out) i...  9.12 us
    all_to_all x1, waiting for transfers between devices, body(): sums = lax.all_to_all(sums, SECOND, 0, 0, tiled=True)  6.56 us
    ppermute x8, starting transfers between devices, exchange(): bo = lax.ppermute(b, 'slab', swap(lax.axis_size('slab'), 1))  5.29 us
  transfers between devices with their start and end apart: 17, of which 1 were waited for; matrix products, arithmetic and copies ran while one was open for 0% of the time, Pallas kernels for 1%

profile of v4, /device:TPU:1, one launch (start us, length us, event | category | flops | bytes accessed | tf_op | source)
XLA Modules:
  0.0 150.2 jit_solution(15928785171724146376)
XLA Ops:
  0.6 1.4 start.1
  2.0 4.5 %collective-permute-start = (f32[24,128]{1,0:T(8,128)S(1)}, f32[24,128]{1,0:T(8,128)S(1)}, u32[]{:S(2)}, u32[]{:S(2)}) collective-permute-start(f32[24,128]{1,0:T(8,128)S(1)} %get-tuple-element.48), channel_id=1, source_target_pairs={{1,2},{2,1},{3,4},{4,3},{5,6},{6,5},{7,8},{8,7},{9,10},{10,9},{11,... | collective-permute-start | bytes 36872 | tf_op jit(solution)/shard_map/ppermute | solution.py:278
  6.5 0.7 collective-permute-start.1
  7.2 11.8 %all-gather = f32[192,128]{1,0:T(8,128)S(1)} all-gather(f32[48,128]{1,0:T(8,128)S(1)} %get-tuple-element.50), channel_id=2, replica_groups={{0,1,64,65},{2,3,66,67},{4,5,68,69},{6,7,70,71},{8,9,72,73},{10,11,74,7..., dimensions={0}, use_global_device_ids=true | all-gather | bytes 122880 | tf_op jit(solution)/shard_map/all_gather | solution.py:279
  19.5 1.9 %collective-permute-start.2 = (f32[8,128]{1,0:T(8,128)S(1)}, f32[8,128]{1,0:T(8,128)S(1)}, u32[]{:S(2)}, u32[]{:S(2)}) collective-permute-start(f32[8,128]{1,0:T(8,128)S(1)} %get-tuple-element.52), channel_id=1, source_target_pairs={{1,2},{2,1},{3,4},{4,3},{5,6},{6,5},{7,8},{8,7},{9,10},{10,9},{11,... | collective-permute-start | bytes 12296 | tf_op jit(solution)/shard_map/ppermute | solution.py:278
  21.4 0.7 collective-permute-start.3
  22.1 9.2 %all-gather.1 = f32[32,128]{1,0:T(8,128)S(1)} all-gather(f32[8,128]{1,0:T(8,128)S(1)} %get-tuple-element.54), channel_id=3, replica_groups={{0,1,64,65},{2,3,66,67},{4,5,68,69},{6,7,70,71},{8,9,72,73},{10,11,74,7..., dimensions={0}, use_global_device_ids=true | all-gather | bytes 20480 | tf_op jit(solution)/shard_map/all_gather | solution.py:279
  31.8 2.9 %collective-permute-start.4 = (f32[8,128]{1,0:T(8,128)S(1)}, f32[8,128]{1,0:T(8,128)S(1)}, u32[]{:S(2)}, u32[]{:S(2)}) collective-permute-start(f32[8,128]{1,0:T(8,128)S(1)} %get-tuple-element.56), channel_id=1, source_target_pairs={{1,2},{2,1},{3,4},{4,3},{5,6},{6,5},{7,8},{8,7},{9,10},{10,9},{11,... | collective-permute-start | bytes 12296 | tf_op jit(solution)/shard_map/ppermute | solution.py:278
  35.4 9.2 %all-gather.2 = f32[32,128]{1,0:T(8,128)S(1)} all-gather(f32[8,128]{1,0:T(8,128)S(1)} %get-tuple-element.58), channel_id=4, replica_groups={{0,1,64,65},{2,3,66,67},{4,5,68,69},{6,7,70,71},{8,9,72,73},{10,11,74,7..., dimensions={0}, use_global_device_ids=true | all-gather | bytes 20480 | tf_op jit(solution)/shard_map/all_gather | solution.py:279
  45.1 3.2 %collective-permute-start.6 = (f32[8,128]{1,0:T(8,128)S(1)}, f32[8,128]{1,0:T(8,128)S(1)}, u32[]{:S(2)}, u32[]{:S(2)}) collective-permute-start(f32[8,128]{1,0:T(8,128)S(1)} %get-tuple-element.60), channel_id=1, source_target_pairs={{1,2},{2,1},{3,4},{4,3},{5,6},{6,5},{7,8},{8,7},{9,10},{10,9},{11,... | collective-permute-start | bytes 12296 | tf_op jit(solution)/shard_map/ppermute | solution.py:278
  49.0 8.0 %all-gather.3 = f32[32,128]{1,0:T(8,128)S(1)} all-gather(f32[8,128]{1,0:T(8,128)S(1)} %get-tuple-element.62), channel_id=5, replica_groups={{0,1,64,65},{2,3,66,67},{4,5,68,69},{6,7,70,71},{8,9,72,73},{10,11,74,7..., dimensions={0}, use_global_device_ids=true | all-gather | bytes 20480 | tf_op jit(solution)/shard_map/all_gather | solution.py:279
  57.5 4.0 %collective-permute-start.8 = (f32[8,128]{1,0:T(8,128)S(1)}, f32[8,128]{1,0:T(8,128)S(1)}, u32[]{:S(2)}, u32[]{:S(2)}) collective-permute-start(f32[8,128]{1,0:T(8,128)S(1)} %get-tuple-element.64), channel_id=1, source_target_pairs={{1,2},{2,1},{3,4},{4,3},{5,6},{6,5},{7,8},{8,7},{9,10},{10,9},{11,... | collective-permute-start | bytes 12296 | tf_op jit(solution)/shard_map/ppermute | solution.py:278
  62.2 8.2 %all-gather.4 = f32[32,128]{1,0:T(8,128)S(1)} all-gather(f32[8,128]{1,0:T(8,128)S(1)} %get-tuple-element.66), channel_id=6, replica_groups={{0,1,64,65},{2,3,66,67},{4,5,68,69},{6,7,70,71},{8,9,72,73},{10,11,74,7..., dimensions={0}, use_global_device_ids=true | all-gather | bytes 20480 | tf_op jit(solution)/shard_map/all_gather | solution.py:279
  70.9 3.1 %collective-permute-start.10 = (f32[8,128]{1,0:T(8,128)S(1)}, f32[8,128]{1,0:T(8,128)S(1)}, u32[]{:S(2)}, u32[]{:S(2)}) collective-permute-start(f32[8,128]{1,0:T(8,128)S(1)} %get-tuple-element.68), channel_id=1, source_target_pairs={{1,2},{2,1},{3,4},{4,3},{5,6},{6,5},{7,8},{8,7},{9,10},{10,9},{11,... | collective-permute-start | bytes 12296 | tf_op jit(solution)/shard_map/ppermute | solution.py:278
  74.7 7.7 %all-gather.5 = f32[32,128]{1,0:T(8,128)S(1)} all-gather(f32[8,128]{1,0:T(8,128)S(1)} %get-tuple-element.70), channel_id=7, replica_groups={{0,1,64,65},{2,3,66,67},{4,5,68,69},{6,7,70,71},{8,9,72,73},{10,11,74,7..., dimensions={0}, use_global_device_ids=true | all-gather | bytes 20480 | tf_op jit(solution)/shard_map/all_gather | solution.py:279
  82.9 3.6 %collective-permute-start.12 = (f32[8,128]{1,0:T(8,128)S(1)}, f32[8,128]{1,0:T(8,128)S(1)}, u32[]{:S(2)}, u32[]{:S(2)}) collective-permute-start(f32[8,128]{1,0:T(8,128)S(1)} %get-tuple-element.72), channel_id=1, source_target_pairs={{1,2},{2,1},{3,4},{4,3},{5,6},{6,5},{7,8},{8,7},{9,10},{10,9},{11,... | collective-permute-start | bytes 12296 | tf_op jit(solution)/shard_map/ppermute | solution.py:278
  87.2 8.0 %all-gather.6 = f32[32,128]{1,0:T(8,128)S(1)} all-gather(f32[8,128]{1,0:T(8,128)S(1)} %get-tuple-element.74), channel_id=8, replica_groups={{0,1,64,65},{2,3,66,67},{4,5,68,69},{6,7,70,71},{8,9,72,73},{10,11,74,7..., dimensions={0}, use_global_device_ids=true | all-gather | bytes 20480 | tf_op jit(solution)/shard_map/all_gather | solution.py:279
  95.7 3.3 %collective-permute-start.14 = (f32[8,128]{1,0:T(8,128)S(1)}, f32[8,128]{1,0:T(8,128)S(1)}, u32[]{:S(2)}, u32[]{:S(2)}) collective-permute-start(f32[8,128]{1,0:T(8,128)S(1)} %get-tuple-element.76), channel_id=1, source_target_pairs={{1,2},{2,1},{3,4},{4,3},{5,6},{6,5},{7,8},{8,7},{9,10},{10,9},{11,... | collective-permute-start | bytes 12296 | tf_op jit(solution)/shard_map/ppermute | solution.py:278
  99.6 7.5 %all-gather.7 = f32[32,128]{1,0:T(8,128)S(1)} all-gather(f32[8,128]{1,0:T(8,128)S(1)} %get-tuple-element.78), channel_id=9, replica_groups={{0,1,64,65},{2,3,66,67},{4,5,68,69},{6,7,70,71},{8,9,72,73},{10,11,74,7..., dimensions={0}, use_global_device_ids=true | all-gather | bytes 20480 | tf_op jit(solution)/shard_map/all_gather | solution.py:279
  107.7 15.9 %all_to_all.10.sums_ref = f32[24,1,128]{2,1,0:T(1,128)S(1)} all-to-all(f32[24,1,128]{2,1,0:T(1,128)S(1)} %step_7.1), channel_id=1, replica_groups=mesh['slab'=12,'sub_0'=8,'sub_1'=4,'sub_2'=2] {'slab','sub_2'}, dimensions={0} | all-to-all | bytes 24576 | tf_op jit(solution)/shard_map/all_to_all | solution.py:349
  124.2 16.4 %all-to-all-start.1 = ((f32[32,1,128]{2,1,0:T(1,128)}), f32[32,1,128]{2,1,0:T(1,128)S(1)}, u32[]{:S(2)}, u32[]{:S(2)}) async-start(f32[32,1,128]{2,1,0:T(1,128)} %regroup.1), calls=%async_computation.1 | async-start | bytes 32768 | tf_op jit(solution)/shard_map/all_to_all | solution.py:351
  140.6 2.0 %blocks_out.1.raw_ref = f32[18,26,512]{2,1,0:T(8,128)S(1)} custom-call(f32[9,32,512]{2,1,0:T(8,128)S(1)} %get-tuple-element.43.refs_0_.scaled_ref, s32[32,512]{1,0:T(8,128)S(1)} %get-tuple-element.44.refs_1_.index_ref, f32[24,512]{1,0:T(8,128)S(1)} %get-tuple-element.79.table_ref, s32[4,128]{1,0:T(4,128)S(1)} %get-tuple-element.46.refs_3_.side_ref, ...), custom_call_target="tpu_custom_call" | custom-call | tf_op jit(solution)/shard_map/blocks_out/pallas_call | solution.py:239
  142.6 6.6 %all-to-all-done.1.sums_ref = f32[32,1,128]{2,1,0:T(1,128)S(1)} async-done(((f32[32,1,128]{2,1,0:T(1,128)}), f32[32,1,128]{2,1,0:T(1,128)S(1)}, u32[]{:S(2)}, u32[]{:S(2)}) %all-to-all-start.1) | async-done | bytes 16416 | tf_op jit(solution)/shard_map/all_to_all | solution.py:351
  149.2 1.0 finish.1
  (31 shorter events, 8.8 us)
Async XLA Ops:
  2.0 17.0 %collective-permute-start = (f32[24,128]{1,0:T(8,128)S(1)}, f32[24,128]{1,0:T(8,128)S(1)}, u32[]{:S(2)}, u32[]{:S(2)}) collective-permute-start(f32[24,128]{1,0:T(8,128)S(1)} %get-tuple-element.48), channel_id=1, source_target_pairs={{1,2},{2,1},{3,4},{4,3},{5,6},{6,5},{7,8},{8,7},{9,10},{10,9},{11,... | collective-permute-start | bytes 36872 | tf_op jit(solution)/shard_map/ppermute | solution.py:278
  6.5 12.5 %collective-permute-start.1 = (f32[24,128]{1,0:T(8,128)S(1)}, f32[24,128]{1,0:T(8,128)S(1)}, u32[]{:S(2)}, u32[]{:S(2)}) collective-permute-start(f32[24,128]{1,0:T(8,128)S(1)} %get-tuple-element.49), channel_id=1, source_target_pairs={{64,128},{128,64},{192,256},{256,192},{320,384},{384,320},{448,512... | collective-permute-start | bytes 36872 | tf_op jit(solution)/shard_map/ppermute | solution.py:277
  19.5 11.8 %collective-permute-start.2 = (f32[8,128]{1,0:T(8,128)S(1)}, f32[8,128]{1,0:T(8,128)S(1)}, u32[]{:S(2)}, u32[]{:S(2)}) collective-permute-start(f32[8,128]{1,0:T(8,128)S(1)} %get-tuple-element.52), channel_id=1, source_target_pairs={{1,2},{2,1},{3,4},{4,3},{5,6},{6,5},{7,8},{8,7},{9,10},{10,9},{11,... | collective-permute-start | bytes 12296 | tf_op jit(solution)/shard_map/ppermute | solution.py:278
  21.4 9.9 %collective-permute-start.3 = (f32[8,128]{1,0:T(8,128)S(1)}, f32[8,128]{1,0:T(8,128)S(1)}, u32[]{:S(2)}, u32[]{:S(2)}) collective-permute-start(f32[8,128]{1,0:T(8,128)S(1)} %get-tuple-element.53), channel_id=1, source_target_pairs={{64,128},{128,64},{192,256},{256,192},{320,384},{384,320},{448,512... | collective-permute-start | bytes 12296 | tf_op jit(solution)/shard_map/ppermute | solution.py:277
  31.8 12.8 %collective-permute-start.4 = (f32[8,128]{1,0:T(8,128)S(1)}, f32[8,128]{1,0:T(8,128)S(1)}, u32[]{:S(2)}, u32[]{:S(2)}) collective-permute-start(f32[8,128]{1,0:T(8,128)S(1)} %get-tuple-element.56), channel_id=1, source_target_pairs={{1,2},{2,1},{3,4},{4,3},{5,6},{6,5},{7,8},{8,7},{9,10},{10,9},{11,... | collective-permute-start | bytes 12296 | tf_op jit(solution)/shard_map/ppermute | solution.py:278
  34.7 9.9 %collective-permute-start.5 = (f32[8,128]{1,0:T(8,128)S(1)}, f32[8,128]{1,0:T(8,128)S(1)}, u32[]{:S(2)}, u32[]{:S(2)}) collective-permute-start(f32[8,128]{1,0:T(8,128)S(1)} %get-tuple-element.57), channel_id=1, source_target_pairs={{64,128},{128,64},{192,256},{256,192},{320,384},{384,320},{448,512... | collective-permute-start | bytes 12296 | tf_op jit(solution)/shard_map/ppermute | solution.py:277
  45.1 11.9 %collective-permute-start.6 = (f32[8,128]{1,0:T(8,128)S(1)}, f32[8,128]{1,0:T(8,128)S(1)}, u32[]{:S(2)}, u32[]{:S(2)}) collective-permute-start(f32[8,128]{1,0:T(8,128)S(1)} %get-tuple-element.60), channel_id=1, source_target_pairs={{1,2},{2,1},{3,4},{4,3},{5,6},{6,5},{7,8},{8,7},{9,10},{10,9},{11,... | collective-permute-start | bytes 12296 | tf_op jit(solution)/shard_map/ppermute | solution.py:278
  48.3 8.7 %collective-permute-start.7 = (f32[8,128]{1,0:T(8,128)S(1)}, f32[8,128]{1,0:T(8,128)S(1)}, u32[]{:S(2)}, u32[]{:S(2)}) collective-permute-start(f32[8,128]{1,0:T(8,128)S(1)} %get-tuple-element.61), channel_id=1, source_target_pairs={{64,128},{128,64},{192,256},{256,192},{320,384},{384,320},{448,512... | collective-permute-start | bytes 12296 | tf_op jit(solution)/shard_map/ppermute | solution.py:277
  57.5 12.9 %collective-permute-start.8 = (f32[8,128]{1,0:T(8,128)S(1)}, f32[8,128]{1,0:T(8,128)S(1)}, u32[]{:S(2)}, u32[]{:S(2)}) collective-permute-start(f32[8,128]{1,0:T(8,128)S(1)} %get-tuple-element.64), channel_id=1, source_target_pairs={{1,2},{2,1},{3,4},{4,3},{5,6},{6,5},{7,8},{8,7},{9,10},{10,9},{11,... | collective-permute-start | bytes 12296 | tf_op jit(solution)/shard_map/ppermute | solution.py:278
  61.5 8.9 %collective-permute-start.9 = (f32[8,128]{1,0:T(8,128)S(1)}, f32[8,128]{1,0:T(8,128)S(1)}, u32[]{:S(2)}, u32[]{:S(2)}) collective-permute-start(f32[8,128]{1,0:T(8,128)S(1)} %get-tuple-element.65), channel_id=1, source_target_pairs={{64,128},{128,64},{192,256},{256,192},{320,384},{384,320},{448,512... | collective-permute-start | bytes 12296 | tf_op jit(solution)/shard_map/ppermute | solution.py:277
  70.9 11.5 %collective-permute-start.10 = (f32[8,128]{1,0:T(8,128)S(1)}, f32[8,128]{1,0:T(8,128)S(1)}, u32[]{:S(2)}, u32[]{:S(2)}) collective-permute-start(f32[8,128]{1,0:T(8,128)S(1)} %get-tuple-element.68), channel_id=1, source_target_pairs={{1,2},{2,1},{3,4},{4,3},{5,6},{6,5},{7,8},{8,7},{9,10},{10,9},{11,... | collective-permute-start | bytes 12296 | tf_op jit(solution)/shard_map/ppermute | solution.py:278
  74.0 8.4 %collective-permute-start.11 = (f32[8,128]{1,0:T(8,128)S(1)}, f32[8,128]{1,0:T(8,128)S(1)}, u32[]{:S(2)}, u32[]{:S(2)}) collective-permute-start(f32[8,128]{1,0:T(8,128)S(1)} %get-tuple-element.69), channel_id=1, source_target_pairs={{64,128},{128,64},{192,256},{256,192},{320,384},{384,320},{448,512... | collective-permute-start | bytes 12296 | tf_op jit(solution)/shard_map/ppermute | solution.py:277
  82.9 12.3 %collective-permute-start.12 = (f32[8,128]{1,0:T(8,128)S(1)}, f32[8,128]{1,0:T(8,128)S(1)}, u32[]{:S(2)}, u32[]{:S(2)}) collective-permute-start(f32[8,128]{1,0:T(8,128)S(1)} %get-tuple-element.72), channel_id=1, source_target_pairs={{1,2},{2,1},{3,4},{4,3},{5,6},{6,5},{7,8},{8,7},{9,10},{10,9},{11,... | collective-permute-start | bytes 12296 | tf_op jit(solution)/shard_map/ppermute | solution.py:278
  86.5 8.6 %collective-permute-start.13 = (f32[8,128]{1,0:T(8,128)S(1)}, f32[8,128]{1,0:T(8,128)S(1)}, u32[]{:S(2)}, u32[]{:S(2)}) collective-permute-start(f32[8,128]{1,0:T(8,128)S(1)} %get-tuple-element.73), channel_id=1, source_target_pairs={{64,128},{128,64},{192,256},{256,192},{320,384},{384,320},{448,512... | collective-permute-start | bytes 12296 | tf_op jit(solution)/shard_map/ppermute | solution.py:277
  95.7 11.5 %collective-permute-start.14 = (f32[8,128]{1,0:T(8,128)S(1)}, f32[8,128]{1,0:T(8,128)S(1)}, u32[]{:S(2)}, u32[]{:S(2)}) collective-permute-start(f32[8,128]{1,0:T(8,128)S(1)} %get-tuple-element.76), channel_id=1, source_target_pairs={{1,2},{2,1},{3,4},{4,3},{5,6},{6,5},{7,8},{8,7},{9,10},{10,9},{11,... | collective-permute-start | bytes 12296 | tf_op jit(solution)/shard_map/ppermute | solution.py:278
  98.9 8.2 %collective-permute-start.15 = (f32[8,128]{1,0:T(8,128)S(1)}, f32[8,128]{1,0:T(8,128)S(1)}, u32[]{:S(2)}, u32[]{:S(2)}) collective-permute-start(f32[8,128]{1,0:T(8,128)S(1)} %get-tuple-element.77), channel_id=1, source_target_pairs={{64,128},{128,64},{192,256},{256,192},{320,384},{384,320},{448,512... | collective-permute-start | bytes 12296 | tf_op jit(solution)/shard_map/ppermute | solution.py:277
  124.2 25.0 %all-to-all-start.1 = ((f32[32,1,128]{2,1,0:T(1,128)}), f32[32,1,128]{2,1,0:T(1,128)S(1)}, u32[]{:S(2)}, u32[]{:S(2)}) async-start(f32[32,1,128]{2,1,0:T(1,128)} %regroup.1), calls=%async_computation.1 | async-start | bytes 32768 | tf_op jit(solution)/shard_map/all_to_all | solution.py:351
